TPU v7x, 32 devices: a whole 2x2x4 slice. The times are simulated.
32 devices in a mesh: leaf: 8 (over z, x), rhs: 4 (over y, core).
Axes of the slice: x: 2, y: 2, z: 4, core: 2. Of those that a mesh axis runs over, the one named last changes fastest.
Arguments:
- right_sides: bfloat16 [8192, 4096], P('leaf', 'rhs'), may hold values from -6 to 6
- leaf_inverse: bfloat16 [8192, 1024], P(('leaf', 'rhs')), may hold values from -0.1875 to 0.1875
- project_factors: bfloat16 [3, 8192, 128], P(None, 'leaf'), may hold values from -0.1875 to 0.1875
- correct_factors: bfloat16 [3, 8192, 128], P(None, 'leaf'), may hold values from -0.5 to 0.5
- coupling_first: bfloat16 [4, 256, 256], P(None, 'rhs'), may hold values from -0.375 to 0.375
- coupling_second: bfloat16 [2, 256, 256], P(None, 'rhs'), may hold values from -0.375 to 0.375
- coupling_third: bfloat16 [1, 256, 256], P(None, 'rhs'), may hold values from -0.375 to 0.375
Outputs:
- solution: bfloat16 [8192, 4096], P('leaf', 'rhs')
All inputs are finite; a program needn't handle non-finite values.
Results may differ from a plain program's by a relative error of at most 0.014.
Values may be sent and summed in bfloat16 or wider, within the bound.
A program may use at most 64 MiB of HBM per device.

v0:
```python
import functools

import jax
import jax.numpy as jnp
from jax import lax
from jax.experimental import pallas as pl
from jax.experimental.pallas import tpu as pltpu
from jax.sharding import PartitionSpec as P

LEVELS = 3
CHUNKS = 4
BF = jnp.bfloat16
F32 = jnp.float32


def mm(a, b):
    return jnp.dot(a, b, preferred_element_type=F32)


def bit_of(index, stride):
    return lax.rem(lax.div(index, stride), 2)


def flip(index, stride):
    return index + stride * (1 - 2 * bit_of(index, stride))


def kernel(
    b_hbm, a_hbm, p_hbm, c_hbm, w0_hbm, w1_hbm, w2_hbm, out_v,
    b_v, a_v, p_v, pt_v, c_v, w_v, g_v, qf, q_s, q_r, q_v,
    stack, p0f, p0_s, p0_r, p1f, p1_s, p1_r, s1_s, s1_r, p2f, p2_s, p2_r,
    s2_s, s2_r, t2_s, t2_r, a_cat, start,
    lsem, ssem, rsem,
):
    i = lax.axis_index("leaf")
    r = lax.axis_index("rhs")
    blk = a_hbm.shape[0]
    depth = a_hbm.shape[1]
    rows = b_hbm.shape[0]
    cols = b_hbm.shape[1]
    rank = p_hbm.shape[2]
    cw = cols // CHUNKS
    half = depth // 2
    mate = {"rhs": flip(r, 1)}
    across = {"rhs": flip(r, 2)}
    sib = {"leaf": flip(i, 1)}
    near = {"leaf": flip(i, 2)}
    far = {"leaf": flip(i, 4)}
    diag = {"leaf": flip(flip(i, 1), 2)}
    sides = [bit_of(i, 1), bit_of(i, 2), bit_of(i, 4)]
    core = bit_of(r, 1)
    chip = bit_of(r, 2)

    count = [0]
    copies = []

    def send(src, dst, to):
        k = count[0]
        count[0] += 1
        copy = pltpu.make_async_remote_copy(
            src_ref=src, dst_ref=dst, send_sem=ssem.at[k], recv_sem=rsem.at[k],
            device_id=to, device_id_type=pl.DeviceIdType.MESH,
        )
        copy.start()
        copies.append(copy)
        return copy

    nloc = [0]

    def fetch(src, dst):
        copy = pltpu.make_async_copy(src, dst, lsem.at[nloc[0]])
        nloc[0] += 1
        copy.start()
        return copy

    def block(which):
        return pl.ds(pl.multiple_of(which * blk, blk), blk)

    la = fetch(a_hbm, a_v.at[block(r), :])
    lw = [
        fetch(w_hbm.at[lax.div(i, 2 << level)], w_v.at[level, r])
        for level, w_hbm in enumerate((w0_hbm, w1_hbm, w2_hbm))
    ]
    lp = [fetch(p_hbm.at[l], p_v.at[:, pl.ds(l * rank, rank)]) for l in range(LEVELS)]
    lc = [fetch(c_hbm.at[l], c_v.at[:, pl.ds(l * rank, rank)]) for l in range(LEVELS)]
    lb = fetch(b_hbm, b_v)

    barrier = pltpu.get_barrier_semaphore()
    for to in (mate, across, sib, near, far, diag):
        pl.semaphore_signal(barrier, inc=1, device_id=to, device_id_type=pl.DeviceIdType.MESH)
    lp[0].wait()
    pt_v[0] = p_v[:, pl.ds(0, rank)].T
    pl.semaphore_wait(barrier, 6)

    la.wait()
    half_cols = pl.ds(pl.multiple_of(core * half, half), half)
    rest_cols = pl.ds(pl.multiple_of((1 - core) * half, half), half)
    a_mate = send(a_v.at[block(r), rest_cols], a_v.at[block(r), rest_cols], mate)
    a_mate2 = send(a_v.at[block(r), half_cols], a_v.at[block(r), half_cols], mate)
    for copy in lw:
        copy.wait()
    w_across = [send(w_v.at[0, r], w_v.at[0, r], across)]
    w_mate = send(w_v.at[:, r], w_v.at[:, r], mate)
    a_mate.wait_recv()
    pair_rows = pl.ds(pl.multiple_of(chip * 2 * blk, 2 * blk), 2 * blk)
    q_across = []
    for l in range(LEVELS):
        if l > 0:
            lp[l].wait()
            pt_v[l] = p_v[:, pl.ds(l * rank, rank)].T
        part = mm(pt_v[l, :, pair_rows], a_v[pair_rows, half_cols])
        qf[l] = part
        q_s[l] = part.astype(BF)
        q_across.append(send(q_s.at[l], q_r.at[l], across))
    for l in range(1, LEVELS):
        w_across.append(send(w_v.at[l, r], w_v.at[l, r], across))
    pieces = 4
    piece = blk // pieces

    def piece_rows(which, k):
        return pl.ds(pl.multiple_of(which * blk + k * piece, piece), piece)

    a_across = [
        send(a_v.at[piece_rows(r, k), :], a_v.at[piece_rows(r, k), :], across)
        for k in range(pieces)
    ]
    for copy in lc:
        copy.wait()
    own_lanes = pl.ds(pl.multiple_of(sides[0] * rank, rank), rank)
    g_send = []
    for n, (l, k) in enumerate(((1, 0), (2, 0), (2, 1))):
        g_v[n, :, own_lanes] = mm(pt_v[l], c_v[:, pl.ds(k * rank, rank)]).astype(BF)
        g_send.append(send(g_v.at[n, :, own_lanes], g_v.at[n, :, own_lanes], sib))

    def relay_w(l):
        w_across[l].wait_recv()
        w_relay.append(send(w_v.at[l, flip(r, 2)], w_v.at[l, flip(r, 2)], mate))

    w_relay = []
    relay_w(0)
    lb.wait()

    def finish_q(l):
        q_across[l].wait_recv()
        q_v[l, core] = (qf[l] + q_r[l].astype(F32)).astype(BF)
        return send(q_v.at[l, core], q_v.at[l, core], mate)

    def project(l, c):
        own = pl.ds(c * cw, cw)
        return mm(q_v[l, 0], b_v[pl.ds(0, half), own]) + mm(q_v[l, 1], b_v[pl.ds(half, half), own])

    def start_rows(which):
        for c in range(CHUNKS):
            own = pl.ds(c * cw, cw)
            start[block(which), own] = mm(a_v[block(which), :], b_v[:, own]).astype(BF)

    def weight(l, other):
        row = pl.ds(pl.multiple_of(sides[l] * 2, 2), 2)
        column = (1 - sides[l]) if other else sides[l]
        lanes = pl.ds(pl.multiple_of(column * rank, rank), rank)
        return w_v[l, row, :, lanes].reshape(rank, rank)

    hw = cw // 2
    keep = pl.ds(pl.multiple_of(sides[0] * hw, hw), hw)
    give = pl.ds(pl.multiple_of((1 - sides[0]) * hw, hw), hw)
    exchange = []
    for l, (f_v, s_v, r_v) in enumerate(((p0f, p0_s, p0_r), (p1f, p1_s, p1_r), (p2f, p2_s, p2_r))):
        copy = finish_q(l)
        if l == 2:
            a_mate2.wait_recv()
            start_rows(r)
        copy.wait_recv()
        sends = []
        for c in range(CHUNKS):
            part = project(l, c)
            if l > 0:
                f_v[c] = part
            if l < 2:
                s_v[c] = part.astype(BF)
            else:
                s_v[c] = f_v[c, :, give].astype(BF)
            sends.append(send(s_v.at[c], r_v.at[c], sib))
        exchange.append(sends)
    x0, x1, x2 = exchange
    w_mate.wait_recv()
    w_relay[0].wait_recv()
    for copy in g_send:
        copy.wait_recv()
    mine_rows = pl.ds(pl.multiple_of(sides[0] * rank, rank), rank)
    other_rows = pl.ds(pl.multiple_of((1 - sides[0]) * rank, rank), rank)
    node = w_v[0].reshape(2 * rank, 2 * rank)

    def first(c):
        x0[c].wait_recv()
        stack[c, mine_rows, :] = p0_s[c]
        stack[c, other_rows, :] = p0_r[c]
        both = mm(node, stack[c]).astype(BF)
        stack[c] = both
        a_cat[c, pl.ds(0, rank), :] = stack[c, mine_rows, :]
        p1f[c] = p1f[c] - mm(g_v[0], both)
        p2f[c, :, keep] = p2f[c, :, keep] - mm(g_v[1], stack[c, :, keep])

    z1 = []

    def second_sum(c):
        x1[c].wait_recv()
        s1_s[c] = (p1f[c] + p1_r[c].astype(F32)).astype(BF)
        z1.append(send(s1_s.at[c], s1_r.at[c], near))

    def second(c):
        z1[c].wait_recv()
        a1 = (mm(weight(1, False), s1_s[c]) + mm(weight(1, True), s1_r[c])).astype(BF)
        a_cat[c, pl.ds(rank, rank), :] = a1
        a1 = a_cat[c, pl.ds(rank, rank), keep]
        p2f[c, :, keep] = (
            p2f[c, :, keep] - mm(g_v[2, :, pl.ds(0, rank)], a1) - mm(g_v[2, :, pl.ds(rank, rank)], a1)
        )

    n1 = []

    def third_sum(c):
        x2[c].wait_recv()
        p2f[c, :, keep] = p2f[c, :, keep] + p2_r[c].astype(F32)
        if c % 2 == 1:
            j = c // 2
            s2_s[j] = p2f[2 * j + 1 - sides[1], :, keep].astype(BF)
            n1.append(send(s2_s.at[j], s2_r.at[j], near))

    f1 = []

    def third_far(j):
        n1[j].wait_recv()
        t2_s[j] = (p2f[2 * j + sides[1], :, keep] + s2_r[j].astype(F32)).astype(BF)
        f1.append(send(t2_s.at[j], t2_r.at[j], far))

    n2 = []

    def third(j):
        f1[j].wait_recv()
        mine = 2 * j + sides[1]
        where = pl.ds(2 * rank, rank)
        a_cat[mine, where, keep] = (
            mm(weight(2, False), t2_s[j]) + mm(weight(2, True), t2_r[j])
        ).astype(BF)
        spot = a_cat.at[mine, where, keep]
        n2.append([send(spot, spot, to) for to in (diag, sib, near)])

    relay = []

    def relay_piece(k):
        a_across[k].wait_recv()
        where = piece_rows(flip(r, 2), k)
        relay.append(send(a_v.at[where, :], a_v.at[where, :], mate))

    def finish(c):
        own = pl.ds(c * cw, cw)
        for n in range(4):
            band = pl.ds(n * (rows // 4), rows // 4)
            out_v[band, own] = (start[band, own].astype(F32) - mm(c_v[band, :], a_cat[c])).astype(BF)

    relay_w(1)
    relay_w(2)
    start_rows(flip(r, 1))
    for c in range(CHUNKS):
        first(c)
    for c in range(CHUNKS):
        second_sum(c)
        if c == 1:
            w_relay[1].wait_recv()
            w_relay[2].wait_recv()
    second(0)
    second(1)
    third_sum(0)
    third_sum(1)
    for c in range(2, CHUNKS):
        second(c)
        third_sum(c)
    third_far(0)
    for k in range(pieces):
        relay_piece(k)
    for j in range(1, CHUNKS // 2):
        third_far(j)
    start_rows(flip(r, 2))
    for copy in relay:
        copy.wait_recv()
    start_rows(flip(flip(r, 2), 1))
    for j in range(CHUNKS // 2):
        third(j)
    for j in range(CHUNKS // 2):
        for copy in n2[j]:
            copy.wait_recv()
        finish(2 * j)
        finish(2 * j + 1)
    for copy in copies:
        copy.wait_send()


def local(right_sides, leaf_inverse, project_factors, correct_factors, *couplings):
    rows, cols = right_sides.shape
    blk, depth = leaf_inverse.shape
    levels, _, rank = project_factors.shape
    parts = lax.axis_size("rhs")
    cw = cols // CHUNKS
    full = lambda dtype: pltpu.VMEM((CHUNKS, rank, cw), dtype)
    thin = lambda dtype: pltpu.VMEM((CHUNKS, rank, cw // 2), dtype)
    part = lambda dtype: pltpu.VMEM((CHUNKS // 2, rank, cw // 2), dtype)
    copies = 96
    any_spec = pl.BlockSpec(memory_space=pltpu.HBM)
    return pl.pallas_call(
        kernel,
        out_shape=jax.ShapeDtypeStruct((rows, cols), BF),
        in_specs=[any_spec] * 7,
        out_specs=pl.BlockSpec(memory_space=pltpu.VMEM),
        scratch_shapes=[
            pltpu.VMEM((rows, cols), BF),
            pltpu.VMEM((rows, depth), BF),
            pltpu.VMEM((rows, levels * rank), BF),
            pltpu.VMEM((levels, rank, rows), BF),
            pltpu.VMEM((rows, levels * rank), BF),
            pltpu.VMEM((levels, parts) + couplings[0].shape[1:], BF),
            pltpu.VMEM((3, rank, 2 * rank), BF),
            pltpu.VMEM((levels, rank, depth // 2), F32),
            pltpu.VMEM((levels, rank, depth // 2), BF),
            pltpu.VMEM((levels, rank, depth // 2), BF),
            pltpu.VMEM((levels, 2, rank, depth // 2), BF),
            pltpu.VMEM((CHUNKS, 2 * rank, cw), BF),
            full(F32), full(BF), full(BF), full(F32), full(BF), full(BF), full(BF), full(BF),
            full(F32), thin(BF), thin(BF),
            part(BF), part(BF), part(BF), part(BF),
            pltpu.VMEM((CHUNKS, levels * rank, cw), BF),
            pltpu.VMEM((rows, cols), BF),
            pltpu.SemaphoreType.DMA((16,)),
            pltpu.SemaphoreType.DMA((copies,)),
            pltpu.SemaphoreType.DMA((copies,)),
        ],
        compiler_params=pltpu.CompilerParams(
            collective_id=0, has_side_effects=True, vmem_limit_bytes=48 * 1024 * 1024
        ),
    )(*(
        pltpu.with_memory_space_constraint(x, pltpu.HBM)
        for x in (right_sides, leaf_inverse, project_factors, correct_factors, *couplings)
    ))


def solution(mesh):
    in_specs = (
        P("leaf", "rhs"),
        P(("leaf", "rhs"), None),
        P(None, "leaf", None),
        P(None, "leaf", None),
        P(None, "rhs", None),
        P(None, "rhs", None),
        P(None, "rhs", None),
    )
    out_specs = P("leaf", "rhs")
    return jax.shard_map(local, mesh=mesh, in_specs=in_specs, out_specs=out_specs, check_vma=False)
```

profile of v0, /device:TPU:0, one launch (start us, length us, event | category | flops | bytes accessed | tf_op | source)
XLA Modules:
  0.0 44.9 jit_solution(14080758983143520459)
XLA Ops:
  0.0 43.6 %shard_map.73 = bf16[1024,1024]{1,0:T(8,128)(2,1)S(1)} custom-call(bf16[1024,1024]{1,0:T(8,128)(2,1)} %b_hbm.1, bf16[256,1024]{1,0:T(8,128)(2,1)} %a_hbm.1, bf16[3,1024,128]{2,1,0:T(8,128)(2,1)} %p_hbm.1, bf16[3,1024,128]{2,1,0:T(8,128)(2,1)} %c_hbm.1, bf16[4,64,256]{2,1,0:T(8,128)(2,1)} %w0_hbm.1, bf16[2,64,256]{2,1,0:T(8,128)(2,1)} %w1_hbm.1, ...), custom_call_target="tpu_custom_call" | custom-call | tf_op jit(solution)/shard_map/pallas_call | solution.py:309
  43.6 1.3 %copy.9 = bf16[1024,1024]{1,0:T(8,128)(2,1)} copy(bf16[1024,1024]{1,0:T(8,128)(2,1)S(1)} %shard_map.73) | data formatting | bytes 4194304
where the time goes:
time: 45.1 us; the launch traced here: 44.9 us
  Pallas kernels  43.6 us (97%)
  local copies, waits for them, and re-layouts  1.32 us (3%)
    pallas_call x1, Pallas kernels, local(): pl.pallas_call(kernel, out_shape=jax.ShapeDtypeStruct((rows, cols), BF),...  43.6 us
    unnamed x1, local copies, waits for them, and re-layouts  1.32 us

commit v1 on v0

v1 whole, which is shorter than its diff:
```python
import jax
import jax.numpy as jnp
from jax import lax
from jax.experimental import pallas as pl
from jax.experimental.pallas import tpu as pltpu
from jax.sharding import PartitionSpec as P

LEVELS = 3
CHUNKS = 4
PIECES = 4
BF = jnp.bfloat16
F32 = jnp.float32


def mm(a, b):
    return jnp.dot(a, b, preferred_element_type=F32)


def bit_of(index, stride):
    return lax.rem(lax.div(index, stride), 2)


def flip(index, stride):
    return index + stride * (1 - 2 * bit_of(index, stride))


def span(which, size):
    return pl.ds(pl.multiple_of(which * size, size), size)


def kernel(
    b_hbm, a_hbm, p_hbm, c_hbm, w0_hbm, w1_hbm, w2_hbm, out_v,
    b_v, a_v, p_v, pt_v, c_v, w_v, g_v, gs_v, h_v, qf, q_s, q_r, q_v,
    pf, st0, p1f, p1_s, p1_r, p2f, x2_s, x2_r, n_s, n_r, st1, st2, a_cat, start, acc,
    lsem, ssem, rsem,
):
    i = lax.axis_index("leaf")
    r = lax.axis_index("rhs")
    blk = a_hbm.shape[0]
    depth = a_hbm.shape[1]
    cols = b_hbm.shape[1]
    rank = p_hbm.shape[2]
    cw = cols // CHUNKS
    hw = cw // 2
    half = depth // 2
    piece = depth // PIECES
    mate = {"rhs": flip(r, 1)}
    across = {"rhs": flip(r, 2)}
    sib = {"leaf": flip(i, 1)}
    near = {"leaf": flip(i, 2)}
    far = {"leaf": flip(i, 4)}
    diag = {"leaf": flip(flip(i, 1), 2)}
    sides = [bit_of(i, 1), bit_of(i, 2), bit_of(i, 4)]
    core = bit_of(r, 1)
    chip = bit_of(r, 2)

    copies = []

    def send(src, dst, to):
        copy = pltpu.make_async_remote_copy(
            src_ref=src, dst_ref=dst, send_sem=ssem.at[0], recv_sem=rsem.at[len(copies)],
            device_id=to, device_id_type=pl.DeviceIdType.MESH,
        )
        copy.start()
        copies.append(copy)
        return copy

    def share(ref, to):
        return send(ref, ref, to)

    nloc = [0]

    def fetch(src, dst):
        copy = pltpu.make_async_copy(src, dst, lsem.at[nloc[0]])
        nloc[0] += 1
        copy.start()
        return copy

    mine = [span(s, rank) for s in sides]
    block = span(r, blk)
    pair_rows = span(chip, 2 * blk)
    other_rows = span(1 - chip, 2 * blk)
    half_cols = span(core, half)
    rest_cols = span(1 - core, half)

    la = fetch(a_hbm, a_v.at[block, :])
    lp = [fetch(p_hbm.at[0], p_v.at[:, pl.ds(0, rank)])]
    lw = [
        fetch(w_hbm.at[lax.div(i, 2 << level)], w_v.at[level, r])
        for level, w_hbm in enumerate((w0_hbm, w1_hbm, w2_hbm))
    ]
    lp += [fetch(p_hbm.at[l], p_v.at[:, pl.ds(l * rank, rank)]) for l in range(1, LEVELS)]
    lc = [fetch(c_hbm.at[l], c_v.at[:, pl.ds(l * rank, rank)]) for l in range(LEVELS)]
    lb = fetch(b_hbm, b_v)

    barrier = pltpu.get_barrier_semaphore()
    for to in (mate, across, sib, near, far, diag):
        pl.semaphore_signal(barrier, inc=1, device_id=to, device_id_type=pl.DeviceIdType.MESH)
    la.wait()
    pl.semaphore_wait(barrier, 6)

    a_mate = share(a_v.at[block, rest_cols], mate)
    for copy in lw:
        copy.wait()
    w_early = [share(w_v.at[l, r, :, mine[l]], across) for l in range(2)]
    a_mate2 = share(a_v.at[block, half_cols], mate)
    w_mate = share(w_v.at[:, r], mate)
    lp[0].wait()
    pt_v[0] = p_v[:, pl.ds(0, rank)].T
    a_mate.wait_recv()
    q_across = []
    for l in range(LEVELS):
        if l > 0:
            lp[l].wait()
            pt_v[l] = p_v[:, pl.ds(l * rank, rank)].T
        part = mm(pt_v[l, :, pair_rows], a_v[pair_rows, half_cols])
        qf[l] = part
        q_s[l] = part.astype(BF)
        q_across.append(send(q_s.at[l], q_r.at[l], across))
    w_late = [share(w_v.at[l, r, :, span(1 - sides[l], rank)], across) for l in range(2)]
    w_late.append(share(w_v.at[2, r], across))
    a_across = [share(a_v.at[block, pl.ds(k * piece, piece)], across) for k in range(PIECES)]

    for copy in lc:
        copy.wait()
    for n, (l, k) in enumerate(((1, 0), (2, 0), (2, 1))):
        g_v[n, :, mine[0]] = mm(pt_v[l], c_v[:, pl.ds(k * rank, rank)]).astype(BF)
    g_send = share(g_v.at[:, :, mine[0]], sib)

    over = flip(r, 2)
    w_relay = []
    for l in range(2):
        w_early[l].wait_recv()
        w_relay.append(share(w_v.at[l, over, :, mine[l]], mate))
    lb.wait()
    a_mate2.wait_recv()
    for c in range(CHUNKS):
        own = pl.ds(c * cw, cw)
        start[:, own] = mm(a_v[pair_rows, :], b_v[:, own])

    def gather_q(l):
        q_across[l].wait_recv()
        q_v[l, core] = (qf[l] + q_r[l].astype(F32)).astype(BF)
        relayed = share(q_v.at[l, core], mate)
        for c in range(CHUNKS):
            pf[c] = mm(q_v[l, core], b_v[half_cols, pl.ds(c * cw, cw)])
        relayed.wait_recv()

    def project(l, c):
        return pf[c] + mm(q_v[l, 1 - core], b_v[rest_cols, pl.ds(c * cw, cw)])

    x0, x1, x2 = {}, {}, {}

    def send0(c):
        x0[c] = share(st0.at[c, mine[0], :], sib)

    def send1(c):
        x1[c] = send(p1_s.at[c], p1_r.at[c], sib)

    gather_q(0)
    for c in range(CHUNKS):
        st0[c, mine[0], :] = project(0, c).astype(BF)
        if c < CHUNKS // 2:
            send0(c)

    w_mate.wait_recv()
    g_send.wait_recv()
    w_relay[0].wait_recv()
    w_cols = w_v[0, :, :, mine[0]].reshape(2 * rank, rank)
    for n in range(2):
        h_v[n] = mm(g_v[n], w_cols).astype(BF)
    pair_sum = g_v[2, :, pl.ds(0, rank)].astype(F32) + g_v[2, :, pl.ds(rank, rank)].astype(F32)
    gs_v[:, mine[1]] = pair_sum.astype(BF)
    gs_send = share(gs_v.at[:, mine[1]], near)

    gather_q(1)
    for c in range(CHUNKS):
        part = project(1, c) - mm(h_v[0], st0[c, mine[0], :])
        p1f[c] = part
        p1_s[c] = part.astype(BF)
        if c < CHUNKS // 2:
            send1(c)

    w_relay[1].wait_recv()
    gs_send.wait_recv()
    h_v[2] = mm(gs_v[...], w_v[1, :, :, mine[1]].reshape(2 * rank, rank)).astype(BF)

    gather_q(2)
    keep = span(sides[0], hw)
    give = span(1 - sides[0], hw)
    for c in range(CHUNKS):
        p2f[c] = project(2, c) - mm(h_v[1], st0[c, mine[0], :]) - mm(h_v[2], p1_s[c])
        x2_s[c] = p2f[c, :, give].astype(BF)
        if c % 2 == 1:
            two = pl.ds(c - 1, 2)
            x2[c // 2] = send(x2_s.at[two], x2_r.at[two], sib)
    for c in range(CHUNKS // 2, CHUNKS):
        send1(c)
    for c in range(CHUNKS // 2, CHUNKS):
        send0(c)
    for l in range(3):
        w_late[l].wait_recv()
        lanes = span(1 - sides[l], rank) if l < 2 else pl.ds(0, 2 * rank)
        w_relay.append(share(w_v.at[l, over, :, lanes], mate))

    def answer_rows(l):
        return w_v[l, pl.ds(pl.multiple_of(sides[l] * 2, 2), 2), :, :].reshape(rank, 2 * rank)

    z1, n1, f1, n2, relay = {}, {}, {}, {}, {}

    def first(c):
        x0[c].wait_recv()
        a_cat[c, pl.ds(0, rank), :] = mm(answer_rows(0), st0[c]).astype(BF)

    def second_sum(c):
        x1[c].wait_recv()
        st1[c, mine[1], :] = (p1f[c] + p1_r[c].astype(F32)).astype(BF)
        z1[c] = share(st1.at[c, mine[1], :], near)

    def second(c):
        z1[c].wait_recv()
        a_cat[c, pl.ds(rank, rank), :] = mm(answer_rows(1), st1[c]).astype(BF)

    def third_near(j):
        x2[j].wait_recv()
        theirs = 2 * j + 1 - sides[1]
        n_s[j] = (p2f[theirs, :, keep] + x2_r[theirs].astype(F32)).astype(BF)
        n1[j] = send(n_s.at[j], n_r.at[j], near)

    def third_far(j):
        n1[j].wait_recv()
        ours = 2 * j + sides[1]
        total = p2f[ours, :, keep] + x2_r[ours].astype(F32) + n_r[j].astype(F32)
        st2[j, mine[2], :] = total.astype(BF)
        f1[j] = share(st2.at[j, mine[2], :], far)

    def third(j):
        f1[j].wait_recv()
        spot = (2 * j + sides[1], pl.ds(2 * rank, rank), keep)
        a_cat[spot] = mm(answer_rows(2), st2[j]).astype(BF)
        n2[j] = [share(a_cat.at[spot], to) for to in (diag, sib, near)]

    def relay_piece(k):
        a_across[k].wait_recv()
        relay[k] = share(a_v.at[span(over, blk), pl.ds(k * piece, piece)], mate)

    def add_pieces(k, count, fresh):
        deep = pl.ds(k * piece, count * piece)
        for c in range(CHUNKS):
            own = pl.ds(c * cw, cw)
            part = mm(a_v[other_rows, deep], b_v[deep, own])
            acc[:, own] = part if fresh else acc[:, own] + part

    def finish_ours(c):
        own = pl.ds(c * cw, cw)
        out_v[pair_rows, own] = (start[:, own] - mm(c_v[pair_rows, :], a_cat[c])).astype(BF)

    def finish_theirs(c):
        own = pl.ds(c * cw, cw)
        deep = pl.ds((PIECES - 1) * piece, piece)
        last = mm(a_v[other_rows, deep], b_v[deep, own]) - mm(c_v[other_rows, :], a_cat[c])
        out_v[other_rows, own] = (acc[:, own] + last).astype(BF)

    second_sum(0)
    second_sum(1)
    third_near(0)
    for l in range(2, 5):
        w_relay[l].wait_recv()
    first(0)
    first(1)
    third_near(1)
    second(0)
    second(1)
    relay_piece(0)
    third_far(0)
    second_sum(2)
    third_far(1)
    relay_piece(1)
    second_sum(3)
    relay[0].wait_recv()
    relay[1].wait_recv()
    add_pieces(0, 2, True)
    third(0)
    first(2)
    second(2)
    third(1)
    relay_piece(2)
    first(3)
    second(3)
    relay[2].wait_recv()
    add_pieces(2, 1, False)
    relay_piece(3)
    for j in range(CHUNKS // 2):
        for copy in n2[j]:
            copy.wait_recv()
        finish_ours(2 * j)
        finish_ours(2 * j + 1)
    relay[3].wait_recv()
    for c in range(CHUNKS):
        finish_theirs(c)
    for copy in copies:
        copy.wait_send()


def local(right_sides, leaf_inverse, project_factors, correct_factors, *couplings):
    rows, cols = right_sides.shape
    blk, depth = leaf_inverse.shape
    levels, _, rank = project_factors.shape
    parts = lax.axis_size("rhs")
    cw = cols // CHUNKS
    whole = lambda dtype: pltpu.VMEM((CHUNKS, rank, cw), dtype)
    thin = lambda dtype: pltpu.VMEM((CHUNKS, rank, cw // 2), dtype)
    part = lambda dtype: pltpu.VMEM((CHUNKS // 2, rank, cw // 2), dtype)
    any_spec = pl.BlockSpec(memory_space=pltpu.HBM)
    return pl.pallas_call(
        kernel,
        out_shape=jax.ShapeDtypeStruct((rows, cols), BF),
        in_specs=[any_spec] * 7,
        out_specs=pl.BlockSpec(memory_space=pltpu.VMEM),
        scratch_shapes=[
            pltpu.VMEM((rows, cols), BF),
            pltpu.VMEM((rows, depth), BF),
            pltpu.VMEM((rows, levels * rank), BF),
            pltpu.VMEM((levels, rank, rows), BF),
            pltpu.VMEM((rows, levels * rank), BF),
            pltpu.VMEM((levels, parts) + couplings[0].shape[1:], BF),
            pltpu.VMEM((3, rank, 2 * rank), BF),
            pltpu.VMEM((rank, 2 * rank), BF),
            pltpu.VMEM((3, rank, rank), BF),
            pltpu.VMEM((levels, rank, depth // 2), F32),
            pltpu.VMEM((levels, rank, depth // 2), BF),
            pltpu.VMEM((levels, rank, depth // 2), BF),
            pltpu.VMEM((levels, 2, rank, depth // 2), BF),
            whole(F32),
            pltpu.VMEM((CHUNKS, 2 * rank, cw), BF),
            whole(F32), whole(BF), whole(BF), whole(F32), thin(BF), thin(BF), part(BF), part(BF),
            pltpu.VMEM((CHUNKS, 2 * rank, cw), BF),
            pltpu.VMEM((CHUNKS // 2, 2 * rank, cw // 2), BF),
            pltpu.VMEM((CHUNKS, levels * rank, cw), BF),
            pltpu.VMEM((rows // 2, cols), F32),
            pltpu.VMEM((rows // 2, cols), F32),
            pltpu.SemaphoreType.DMA((11,)),
            pltpu.SemaphoreType.DMA((1,)),
            pltpu.SemaphoreType.DMA((60,)),
        ],
        compiler_params=pltpu.CompilerParams(
            collective_id=0, has_side_effects=True, vmem_limit_bytes=56 * 1024 * 1024
        ),
    )(*(
        pltpu.with_memory_space_constraint(x, pltpu.HBM)
        for x in (right_sides, leaf_inverse, project_factors, correct_factors, *couplings)
    ))


def solution(mesh):
    in_specs = (
        P("leaf", "rhs"),
        P(("leaf", "rhs"), None),
        P(None, "leaf", None),
        P(None, "leaf", None),
        P(None, "rhs", None),
        P(None, "rhs", None),
        P(None, "rhs", None),
    )
    out_specs = P("leaf", "rhs")
    return jax.shard_map(local, mesh=mesh, in_specs=in_specs, out_specs=out_specs, check_vma=False)
```

time: 45.1 us -> 41.2 us (0.914)
  Pallas kernels: 43.6 us -> 38 us
  local copies, waits for them, and re-layouts: 1.32 us -> 3.08 us
    pallas_call x1, Pallas kernels: 43.6 us -> 38 us  [local(): pl.pallas_call(kernel, out_shape=jax.ShapeDtypeStruct((rows, cols), BF),...]
    unnamed x1, local copies, waits for them, and re-layouts: 1.32 us -> 3.08 us
where the time goes in v1:
time: 41.2 us; the launch traced here: 41.1 us
  Pallas kernels  38 us (92%)
  local copies, waits for them, and re-layouts  3.08 us (7%)
    pallas_call x1, Pallas kernels, local(): pl.pallas_call(kernel, out_shape=jax.ShapeDtypeStruct((rows, cols), BF),...  38 us
    unnamed x1, local copies, waits for them, and re-layouts  3.08 us

profile of v1, /device:TPU:0, one launch (start us, length us, event | category | flops | bytes accessed | tf_op | source)
XLA Modules:
  0.0 41.1 jit_solution(8113827442907593685)
XLA Ops:
  0.0 38.0 %shard_map.73 = bf16[1024,1024]{1,0:T(8,128)(2,1)} custom-call(bf16[1024,1024]{1,0:T(8,128)(2,1)} %b_hbm.1, bf16[256,1024]{1,0:T(8,128)(2,1)} %a_hbm.1, bf16[3,1024,128]{2,1,0:T(8,128)(2,1)} %p_hbm.1, bf16[3,1024,128]{2,1,0:T(8,128)(2,1)} %c_hbm.1, bf16[4,64,256]{2,1,0:T(8,128)(2,1)} %w0_hbm.1, bf16[2,64,256]{2,1,0:T(8,128)(2,1)} %w1_hbm.1, ...), custom_call_target="tpu_custom_call" | custom-call | tf_op jit(solution)/shard_map/pallas_call | solution.py:315
  38.0 3.1 %copy.9 = bf16[1024,1024]{1,0:T(8,128)(2,1)} copy(bf16[1024,1024]{1,0:T(8,128)(2,1)} %shard_map.73) | data formatting | bytes 4194304

commit v2 on v1

--- a/solution.py
+++ b/solution.py
@@ -31,7 +31,7 @@
 def kernel(
     b_hbm, a_hbm, p_hbm, c_hbm, w0_hbm, w1_hbm, w2_hbm, out_v,
     b_v, a_v, p_v, pt_v, c_v, w_v, g_v, gs_v, h_v, qf, q_s, q_r, q_v,
-    pf, st0, p1f, p1_s, p1_r, p2f, x2_s, x2_r, n_s, n_r, st1, st2, a_cat, start, acc,
+    pf, st0, p1f, p1_s, p1_r, p2f, p2_s, p2_r, st1, st2, a_cat, acc,
     lsem, ssem, rsem,
 ):
     i = lax.axis_index("leaf")
@@ -103,8 +103,6 @@
     for copy in lw:
         copy.wait()
     w_early = [share(w_v.at[l, r, :, mine[l]], across) for l in range(2)]
-    a_mate2 = share(a_v.at[block, half_cols], mate)
-    w_mate = share(w_v.at[:, r], mate)
     lp[0].wait()
     pt_v[0] = p_v[:, pl.ds(0, rank)].T
     a_mate.wait_recv()
@@ -117,6 +115,8 @@
         qf[l] = part
         q_s[l] = part.astype(BF)
         q_across.append(send(q_s.at[l], q_r.at[l], across))
+    a_mate2 = share(a_v.at[block, half_cols], mate)
+    w_mate = share(w_v.at[:, r], mate)
     w_late = [share(w_v.at[l, r, :, span(1 - sides[l], rank)], across) for l in range(2)]
     w_late.append(share(w_v.at[2, r], across))
     a_across = [share(a_v.at[block, pl.ds(k * piece, piece)], across) for k in range(PIECES)]
@@ -136,7 +136,7 @@
     a_mate2.wait_recv()
     for c in range(CHUNKS):
         own = pl.ds(c * cw, cw)
-        start[:, own] = mm(a_v[pair_rows, :], b_v[:, own])
+        acc[pair_rows, own] = mm(a_v[pair_rows, :], b_v[:, own])
 
     def gather_q(l):
         q_across[l].wait_recv()
@@ -147,7 +147,7 @@
         relayed.wait_recv()
 
     def project(l, c):
-        return pf[c] + mm(q_v[l, 1 - core], b_v[rest_cols, pl.ds(c * cw, cw)])
+        return pf[c] + mm(q_v[l, 1 - core], b_v[rest_cols, span(c, cw)])
 
     x0, x1, x2 = {}, {}, {}
 
@@ -186,14 +186,14 @@
     h_v[2] = mm(gs_v[...], w_v[1, :, :, mine[1]].reshape(2 * rank, rank)).astype(BF)
 
     gather_q(2)
-    keep = span(sides[0], hw)
-    give = span(1 - sides[0], hw)
-    for c in range(CHUNKS):
-        p2f[c] = project(2, c) - mm(h_v[1], st0[c, mine[0], :]) - mm(h_v[2], p1_s[c])
-        x2_s[c] = p2f[c, :, give].astype(BF)
-        if c % 2 == 1:
-            two = pl.ds(c - 1, 2)
-            x2[c // 2] = send(x2_s.at[two], x2_r.at[two], sib)
+    spot = 2 * sides[1] + sides[0]
+    for n, (to, who) in enumerate(((diag, 3 - spot), (sib, flip(spot, 1)), (near, flip(spot, 2)), (None, spot))):
+        part = project(2, who) - mm(h_v[1], st0[who, mine[0], :]) - mm(h_v[2], p1_s[who])
+        if to is None:
+            p2f[...] = part
+        else:
+            p2_s[n] = part.astype(BF)
+            x2[n] = send(p2_s.at[n], p2_r.at[n], to)
     for c in range(CHUNKS // 2, CHUNKS):
         send1(c)
     for c in range(CHUNKS // 2, CHUNKS):
@@ -206,7 +206,7 @@
     def answer_rows(l):
         return w_v[l, pl.ds(pl.multiple_of(sides[l] * 2, 2), 2), :, :].reshape(rank, 2 * rank)
 
-    z1, n1, f1, n2, relay = {}, {}, {}, {}, {}
+    z1, f1, n2, relay = {}, {}, {}, {}
 
     def first(c):
         x0[c].wait_recv()
@@ -221,24 +221,22 @@
         z1[c].wait_recv()
         a_cat[c, pl.ds(rank, rank), :] = mm(answer_rows(1), st1[c]).astype(BF)
 
-    def third_near(j):
-        x2[j].wait_recv()
-        theirs = 2 * j + 1 - sides[1]
-        n_s[j] = (p2f[theirs, :, keep] + x2_r[theirs].astype(F32)).astype(BF)
-        n1[j] = send(n_s.at[j], n_r.at[j], near)
-
-    def third_far(j):
-        n1[j].wait_recv()
-        ours = 2 * j + sides[1]
-        total = p2f[ours, :, keep] + x2_r[ours].astype(F32) + n_r[j].astype(F32)
-        st2[j, mine[2], :] = total.astype(BF)
-        f1[j] = share(st2.at[j, mine[2], :], far)
+    def third_far():
+        for n in range(3):
+            x2[n].wait_recv()
+        for j in range(2):
+            lanes = pl.ds(j * hw, hw)
+            total = p2f[:, lanes]
+            for n in range(3):
+                total = total + p2_r[n, :, lanes].astype(F32)
+            st2[j, mine[2], :] = total.astype(BF)
+            f1[j] = share(st2.at[j, mine[2], :], far)
 
     def third(j):
         f1[j].wait_recv()
-        spot = (2 * j + sides[1], pl.ds(2 * rank, rank), keep)
-        a_cat[spot] = mm(answer_rows(2), st2[j]).astype(BF)
-        n2[j] = [share(a_cat.at[spot], to) for to in (diag, sib, near)]
+        where = (spot, pl.ds(2 * rank, rank), pl.ds(j * hw, hw))
+        a_cat[where] = mm(answer_rows(2), st2[j]).astype(BF)
+        n2[j] = [share(a_cat.at[where], to) for to in (diag, sib, near)]
 
     def relay_piece(k):
         a_across[k].wait_recv()
@@ -249,55 +247,56 @@
         for c in range(CHUNKS):
             own = pl.ds(c * cw, cw)
             part = mm(a_v[other_rows, deep], b_v[deep, own])
-            acc[:, own] = part if fresh else acc[:, own] + part
-
-    def finish_ours(c):
+            acc[other_rows, own] = part if fresh else acc[other_rows, own] + part
+
+    def take_two(c, rows):
         own = pl.ds(c * cw, cw)
-        out_v[pair_rows, own] = (start[:, own] - mm(c_v[pair_rows, :], a_cat[c])).astype(BF)
-
-    def finish_theirs(c):
+        acc[rows, own] = acc[rows, own] - mm(c_v[rows, pl.ds(0, 2 * rank)], a_cat[c, pl.ds(0, 2 * rank), :])
+
+    def finish(c):
         own = pl.ds(c * cw, cw)
-        deep = pl.ds((PIECES - 1) * piece, piece)
-        last = mm(a_v[other_rows, deep], b_v[deep, own]) - mm(c_v[other_rows, :], a_cat[c])
-        out_v[other_rows, own] = (acc[:, own] + last).astype(BF)
+        last = mm(c_v[:, pl.ds(2 * rank, rank)], a_cat[c, pl.ds(2 * rank, rank), :])
+        out_v[:, own] = (acc[:, own] - last).astype(BF)
 
     second_sum(0)
     second_sum(1)
-    third_near(0)
     for l in range(2, 5):
         w_relay[l].wait_recv()
     first(0)
     first(1)
-    third_near(1)
+    relay_piece(0)
+    third_far()
     second(0)
     second(1)
-    relay_piece(0)
-    third_far(0)
+    take_two(0, pair_rows)
+    take_two(1, pair_rows)
+    relay_piece(1)
+    relay[0].wait_recv()
+    add_pieces(0, 1, True)
+    take_two(0, other_rows)
+    take_two(1, other_rows)
     second_sum(2)
-    third_far(1)
-    relay_piece(1)
+    third(0)
     second_sum(3)
-    relay[0].wait_recv()
-    relay[1].wait_recv()
-    add_pieces(0, 2, True)
-    third(0)
-    first(2)
-    second(2)
     third(1)
     relay_piece(2)
-    first(3)
-    second(3)
+    relay[1].wait_recv()
+    add_pieces(1, 1, False)
+    for c in (2, 3):
+        second(c)
+        first(c)
+        take_two(c, pair_rows)
+        take_two(c, other_rows)
+    relay_piece(3)
     relay[2].wait_recv()
     add_pieces(2, 1, False)
-    relay_piece(3)
-    for j in range(CHUNKS // 2):
+    relay[3].wait_recv()
+    add_pieces(3, 1, False)
+    for j in range(2):
         for copy in n2[j]:
             copy.wait_recv()
-        finish_ours(2 * j)
-        finish_ours(2 * j + 1)
-    relay[3].wait_recv()
     for c in range(CHUNKS):
-        finish_theirs(c)
+        finish(c)
     for copy in copies:
         copy.wait_send()
 
@@ -309,8 +308,6 @@
     parts = lax.axis_size("rhs")
     cw = cols // CHUNKS
     whole = lambda dtype: pltpu.VMEM((CHUNKS, rank, cw), dtype)
-    thin = lambda dtype: pltpu.VMEM((CHUNKS, rank, cw // 2), dtype)
-    part = lambda dtype: pltpu.VMEM((CHUNKS // 2, rank, cw // 2), dtype)
     any_spec = pl.BlockSpec(memory_space=pltpu.HBM)
     return pl.pallas_call(
         kernel,
@@ -333,18 +330,18 @@
             pltpu.VMEM((levels, 2, rank, depth // 2), BF),
             whole(F32),
             pltpu.VMEM((CHUNKS, 2 * rank, cw), BF),
-            whole(F32), whole(BF), whole(BF), whole(F32), thin(BF), thin(BF), part(BF), part(BF),
+            whole(F32), whole(BF), whole(BF),
+            pltpu.VMEM((rank, cw), F32), pltpu.VMEM((3, rank, cw), BF), pltpu.VMEM((3, rank, cw), BF),
             pltpu.VMEM((CHUNKS, 2 * rank, cw), BF),
-            pltpu.VMEM((CHUNKS // 2, 2 * rank, cw // 2), BF),
+            pltpu.VMEM((2, 2 * rank, cw // 2), BF),
             pltpu.VMEM((CHUNKS, levels * rank, cw), BF),
-            pltpu.VMEM((rows // 2, cols), F32),
-            pltpu.VMEM((rows // 2, cols), F32),
+            pltpu.VMEM((rows, cols), F32),
             pltpu.SemaphoreType.DMA((11,)),
             pltpu.SemaphoreType.DMA((1,)),
-            pltpu.SemaphoreType.DMA((60,)),
+            pltpu.SemaphoreType.DMA((52,)),
         ],
         compiler_params=pltpu.CompilerParams(
-            collective_id=0, has_side_effects=True, vmem_limit_bytes=56 * 1024 * 1024
+            collective_id=0, has_side_effects=True, vmem_limit_bytes=40 * 1024 * 1024
         ),
     )(*(
         pltpu.with_memory_space_constraint(x, pltpu.HBM)

time: 41.2 us -> 38.3 us (0.930); the launches traced: 41.1 us -> 37.7 us
  local copies, waits for them, and re-layouts: 3.08 us -> 1.32 us
  Pallas kernels: 38 us -> 36.3 us
    unnamed x1, local copies, waits for them, and re-layouts: 3.08 us -> 1.32 us
    pallas_call x1, Pallas kernels: 38 us -> 36.3 us  [local(): pl.pallas_call(kernel, out_shape=jax.ShapeDtypeStruct((rows, cols), BF),...]
where the time goes in v2:
time: 38.3 us; the launch traced here: 37.7 us
  Pallas kernels  36.3 us (95%)
  local copies, waits for them, and re-layouts  1.32 us (3%)
    pallas_call x1, Pallas kernels, local(): pl.pallas_call(kernel, out_shape=jax.ShapeDtypeStruct((rows, cols), BF),...  36.3 us
    unnamed x1, local copies, waits for them, and re-layouts  1.32 us

profile of v2, /device:TPU:0, one launch (start us, length us, event | category | flops | bytes accessed | tf_op | source)
XLA Modules:
  0.0 37.7 jit_solution(7423496967491205876)
XLA Ops:
  0.0 36.3 %shard_map.73 = bf16[1024,1024]{1,0:T(8,128)(2,1)S(1)} custom-call(bf16[1024,1024]{1,0:T(8,128)(2,1)} %b_hbm.1, bf16[256,1024]{1,0:T(8,128)(2,1)} %a_hbm.1, bf16[3,1024,128]{2,1,0:T(8,128)(2,1)} %p_hbm.1, bf16[3,1024,128]{2,1,0:T(8,128)(2,1)} %c_hbm.1, bf16[4,64,256]{2,1,0:T(8,128)(2,1)} %w0_hbm.1, bf16[2,64,256]{2,1,0:T(8,128)(2,1)} %w1_hbm.1, ...), custom_call_target="tpu_custom_call" | custom-call | tf_op jit(solution)/shard_map/pallas_call | solution.py:312
  36.3 1.3 %copy.9 = bf16[1024,1024]{1,0:T(8,128)(2,1)} copy(bf16[1024,1024]{1,0:T(8,128)(2,1)S(1)} %shard_map.73) | data formatting | bytes 4194304

commit v3 on v2

--- a/solution.py
+++ b/solution.py
@@ -30,8 +30,8 @@
 
 def kernel(
     b_hbm, a_hbm, p_hbm, c_hbm, w0_hbm, w1_hbm, w2_hbm, out_v,
-    b_v, a_v, p_v, pt_v, c_v, w_v, g_v, gs_v, h_v, qf, q_s, q_r, q_v,
-    pf, st0, p1f, p1_s, p1_r, p2f, p2_s, p2_r, st1, st2, a_cat, acc,
+    b_v, a_v, p_v, pt_v, w_v, g_v, gs_v, h_v, qf, q_s, q_r, q_v,
+    pf, st0, p1f, p1_s, p1_r, p2f, p2_s, p2_r, st1, st2, acc,
     lsem, ssem, rsem,
 ):
     i = lax.axis_index("leaf")
@@ -83,15 +83,15 @@
     half_cols = span(core, half)
     rest_cols = span(1 - core, half)
 
-    la = fetch(a_hbm, a_v.at[block, :])
+    la = fetch(a_hbm, a_v.at[block, pl.ds(0, depth)])
     lp = [fetch(p_hbm.at[0], p_v.at[:, pl.ds(0, rank)])]
     lw = [
         fetch(w_hbm.at[lax.div(i, 2 << level)], w_v.at[level, r])
         for level, w_hbm in enumerate((w0_hbm, w1_hbm, w2_hbm))
     ]
     lp += [fetch(p_hbm.at[l], p_v.at[:, pl.ds(l * rank, rank)]) for l in range(1, LEVELS)]
-    lc = [fetch(c_hbm.at[l], c_v.at[:, pl.ds(l * rank, rank)]) for l in range(LEVELS)]
-    lb = fetch(b_hbm, b_v)
+    lc = [fetch(c_hbm.at[l], a_v.at[:, pl.ds(depth + l * rank, rank)]) for l in range(LEVELS)]
+    lb = fetch(b_hbm, b_v.at[pl.ds(0, depth)])
 
     barrier = pltpu.get_barrier_semaphore()
     for to in (mate, across, sib, near, far, diag):
@@ -124,7 +124,7 @@
     for copy in lc:
         copy.wait()
     for n, (l, k) in enumerate(((1, 0), (2, 0), (2, 1))):
-        g_v[n, :, mine[0]] = mm(pt_v[l], c_v[:, pl.ds(k * rank, rank)]).astype(BF)
+        g_v[n, :, mine[0]] = mm(pt_v[l], a_v[:, pl.ds(depth + k * rank, rank)]).astype(BF)
     g_send = share(g_v.at[:, :, mine[0]], sib)
 
     over = flip(r, 2)
@@ -136,7 +136,7 @@
     a_mate2.wait_recv()
     for c in range(CHUNKS):
         own = pl.ds(c * cw, cw)
-        acc[pair_rows, own] = mm(a_v[pair_rows, :], b_v[:, own])
+        acc[pair_rows, own] = mm(a_v[pair_rows, pl.ds(0, depth)], b_v[pl.ds(0, depth), own])
 
     def gather_q(l):
         q_across[l].wait_recv()
@@ -210,7 +210,7 @@
 
     def first(c):
         x0[c].wait_recv()
-        a_cat[c, pl.ds(0, rank), :] = mm(answer_rows(0), st0[c]).astype(BF)
+        b_v[pl.ds(depth, rank), pl.ds(c * cw, cw)] = (-mm(answer_rows(0), st0[c])).astype(BF)
 
     def second_sum(c):
         x1[c].wait_recv()
@@ -219,7 +219,7 @@
 
     def second(c):
         z1[c].wait_recv()
-        a_cat[c, pl.ds(rank, rank), :] = mm(answer_rows(1), st1[c]).astype(BF)
+        b_v[pl.ds(depth + rank, rank), pl.ds(c * cw, cw)] = (-mm(answer_rows(1), st1[c])).astype(BF)
 
     def third_far():
         for n in range(3):
@@ -234,29 +234,25 @@
 
     def third(j):
         f1[j].wait_recv()
-        where = (spot, pl.ds(2 * rank, rank), pl.ds(j * hw, hw))
-        a_cat[where] = mm(answer_rows(2), st2[j]).astype(BF)
-        n2[j] = [share(a_cat.at[where], to) for to in (diag, sib, near)]
+        where = (pl.ds(depth + 2 * rank, rank), span(2 * spot + j, hw))
+        b_v[where] = (-mm(answer_rows(2), st2[j])).astype(BF)
+        n2[j] = [share(b_v.at[where], to) for to in (diag, sib, near)]
 
     def relay_piece(k):
         a_across[k].wait_recv()
         relay[k] = share(a_v.at[span(over, blk), pl.ds(k * piece, piece)], mate)
 
-    def add_pieces(k, count, fresh):
-        deep = pl.ds(k * piece, count * piece)
+    early = depth - piece
+
+    def add_pieces():
         for c in range(CHUNKS):
             own = pl.ds(c * cw, cw)
-            part = mm(a_v[other_rows, deep], b_v[deep, own])
-            acc[other_rows, own] = part if fresh else acc[other_rows, own] + part
-
-    def take_two(c, rows):
+            acc[other_rows, own] = mm(a_v[other_rows, pl.ds(0, early)], b_v[pl.ds(0, early), own])
+
+    def finish(c, rows, start):
         own = pl.ds(c * cw, cw)
-        acc[rows, own] = acc[rows, own] - mm(c_v[rows, pl.ds(0, 2 * rank)], a_cat[c, pl.ds(0, 2 * rank), :])
-
-    def finish(c):
-        own = pl.ds(c * cw, cw)
-        last = mm(c_v[:, pl.ds(2 * rank, rank)], a_cat[c, pl.ds(2 * rank, rank), :])
-        out_v[:, own] = (acc[:, own] - last).astype(BF)
+        deep = pl.ds(start, depth + LEVELS * rank - start)
+        out_v[rows, own] = (acc[rows, own] + mm(a_v[rows, deep], b_v[deep, own])).astype(BF)
 
     second_sum(0)
     second_sum(1)
@@ -266,37 +262,30 @@
     first(1)
     relay_piece(0)
     third_far()
+    relay_piece(1)
+    second_sum(2)
     second(0)
+    second_sum(3)
     second(1)
-    take_two(0, pair_rows)
-    take_two(1, pair_rows)
-    relay_piece(1)
-    relay[0].wait_recv()
-    add_pieces(0, 1, True)
-    take_two(0, other_rows)
-    take_two(1, other_rows)
-    second_sum(2)
+    relay_piece(2)
     third(0)
-    second_sum(3)
     third(1)
-    relay_piece(2)
-    relay[1].wait_recv()
-    add_pieces(1, 1, False)
-    for c in (2, 3):
-        second(c)
-        first(c)
-        take_two(c, pair_rows)
-        take_two(c, other_rows)
+    first(2)
+    first(3)
+    for k in range(3):
+        relay[k].wait_recv()
+    add_pieces()
+    second(2)
     relay_piece(3)
-    relay[2].wait_recv()
-    add_pieces(2, 1, False)
-    relay[3].wait_recv()
-    add_pieces(3, 1, False)
+    second(3)
     for j in range(2):
         for copy in n2[j]:
             copy.wait_recv()
     for c in range(CHUNKS):
-        finish(c)
+        finish(c, pair_rows, depth)
+    relay[3].wait_recv()
+    for c in range(CHUNKS):
+        finish(c, other_rows, early)
     for copy in copies:
         copy.wait_send()
 
@@ -315,11 +304,10 @@
         in_specs=[any_spec] * 7,
         out_specs=pl.BlockSpec(memory_space=pltpu.VMEM),
         scratch_shapes=[
-            pltpu.VMEM((rows, cols), BF),
-            pltpu.VMEM((rows, depth), BF),
+            pltpu.VMEM((depth + levels * rank, cols), BF),
+            pltpu.VMEM((rows, depth + levels * rank), BF),
             pltpu.VMEM((rows, levels * rank), BF),
             pltpu.VMEM((levels, rank, rows), BF),
-            pltpu.VMEM((rows, levels * rank), BF),
             pltpu.VMEM((levels, parts) + couplings[0].shape[1:], BF),
             pltpu.VMEM((3, rank, 2 * rank), BF),
             pltpu.VMEM((rank, 2 * rank), BF),
@@ -334,7 +322,6 @@
             pltpu.VMEM((rank, cw), F32), pltpu.VMEM((3, rank, cw), BF), pltpu.VMEM((3, rank, cw), BF),
             pltpu.VMEM((CHUNKS, 2 * rank, cw), BF),
             pltpu.VMEM((2, 2 * rank, cw // 2), BF),
-            pltpu.VMEM((CHUNKS, levels * rank, cw), BF),
             pltpu.VMEM((rows, cols), F32),
             pltpu.SemaphoreType.DMA((11,)),
             pltpu.SemaphoreType.DMA((1,)),

time: 38.3 us -> 37 us (0.966); the launches traced: 37.7 us -> 36.9 us
  Pallas kernels: 36.3 us -> 35.5 us
    pallas_call x1, Pallas kernels: 36.3 us -> 35.5 us  [local(): pl.pallas_call(kernel, out_shape=jax.ShapeDtypeStruct((rows, cols), BF),...]
where the time goes in v3:
time: 37 us; the launch traced here: 36.9 us
  Pallas kernels  35.5 us (96%)
  local copies, waits for them, and re-layouts  1.32 us (4%)
    pallas_call x1, Pallas kernels, local(): pl.pallas_call(kernel, out_shape=jax.ShapeDtypeStruct((rows, cols), BF),...  35.5 us
    unnamed x1, local copies, waits for them, and re-layouts  1.32 us

profile of v3, /device:TPU:0, one launch (start us, length us, event | category | flops | bytes accessed | tf_op | source)
XLA Modules:
  0.0 36.9 jit_solution(10031173223445003441)
XLA Ops:
  0.0 35.5 %shard_map.73 = bf16[1024,1024]{1,0:T(8,128)(2,1)S(1)} custom-call(bf16[1024,1024]{1,0:T(8,128)(2,1)} %b_hbm.1, bf16[256,1024]{1,0:T(8,128)(2,1)} %a_hbm.1, bf16[3,1024,128]{2,1,0:T(8,128)(2,1)} %p_hbm.1, bf16[3,1024,128]{2,1,0:T(8,128)(2,1)} %c_hbm.1, bf16[4,64,256]{2,1,0:T(8,128)(2,1)} %w0_hbm.1, bf16[2,64,256]{2,1,0:T(8,128)(2,1)} %w1_hbm.1, ...), custom_call_target="tpu_custom_call" | custom-call | tf_op jit(solution)/shard_map/pallas_call | solution.py:301
  35.6 1.3 %copy.9 = bf16[1024,1024]{1,0:T(8,128)(2,1)} copy(bf16[1024,1024]{1,0:T(8,128)(2,1)S(1)} %shard_map.73) | data formatting | bytes 4194304

commit v4 on v3

--- a/solution.py
+++ b/solution.py
@@ -32,7 +32,7 @@
     b_hbm, a_hbm, p_hbm, c_hbm, w0_hbm, w1_hbm, w2_hbm, out_v,
     b_v, a_v, p_v, pt_v, w_v, g_v, gs_v, h_v, qf, q_s, q_r, q_v,
     pf, st0, p1f, p1_s, p1_r, p2f, p2_s, p2_r, st1, st2, acc,
-    lsem, ssem, rsem,
+    lsem, ssem, rsem, msem,
 ):
     i = lax.axis_index("leaf")
     r = lax.axis_index("rhs")
@@ -50,6 +50,7 @@
     near = {"leaf": flip(i, 2)}
     far = {"leaf": flip(i, 4)}
     diag = {"leaf": flip(flip(i, 1), 2)}
+    mid = {"leaf": flip(flip(i, 2), 4)}
     sides = [bit_of(i, 1), bit_of(i, 2), bit_of(i, 4)]
     core = bit_of(r, 1)
     chip = bit_of(r, 2)
@@ -94,10 +95,21 @@
     lb = fetch(b_hbm, b_v.at[pl.ds(0, depth)])
 
     barrier = pltpu.get_barrier_semaphore()
-    for to in (mate, across, sib, near, far, diag):
+    inner = lax.rem(sides[1] + sides[2], 2)
+    for to in (mate, across, sib, near):
         pl.semaphore_signal(barrier, inc=1, device_id=to, device_id_type=pl.DeviceIdType.MESH)
+
+    @pl.when(inner == 1)
+    def _():
+        pl.semaphore_signal(barrier, inc=1, device_id=mid, device_id_type=pl.DeviceIdType.MESH)
+
     la.wait()
-    pl.semaphore_wait(barrier, 6)
+    pl.semaphore_wait(barrier, 4 + inner)
+
+    @pl.when(inner == 1)
+    def _():
+        pl.semaphore_signal(msem, inc=1, device_id=mid, device_id_type=pl.DeviceIdType.MESH)
+
 
     a_mate = share(a_v.at[block, rest_cols], mate)
     for copy in lw:
@@ -187,13 +199,31 @@
 
     gather_q(2)
     spot = 2 * sides[1] + sides[0]
-    for n, (to, who) in enumerate(((diag, 3 - spot), (sib, flip(spot, 1)), (near, flip(spot, 2)), (None, spot))):
+    spots = (3 - spot, flip(spot, 1), flip(spot, 2), spot)
+    team = (diag, sib, near)
+
+    def level_two(n):
+        who = spots[n]
         part = project(2, who) - mm(h_v[1], st0[who, mine[0], :]) - mm(h_v[2], p1_s[who])
-        if to is None:
+        if n == 3:
             p2f[...] = part
         else:
-            p2_s[n] = part.astype(BF)
-            x2[n] = send(p2_s.at[n], p2_r.at[n], to)
+            for h in range(2):
+                p2_s[n, h] = part[:, h * hw:(h + 1) * hw].astype(BF)
+
+    def send2(n, h):
+        x2[n, h] = send(p2_s.at[n, h], p2_r.at[n, h], team[n])
+
+    level_two(0)
+    send2(0, 0)
+    level_two(1)
+    send2(1, 0)
+    send2(0, 1)
+    send2(1, 1)
+    level_two(2)
+    send2(2, 0)
+    send2(2, 1)
+    level_two(3)
     for c in range(CHUNKS // 2, CHUNKS):
         send1(c)
     for c in range(CHUNKS // 2, CHUNKS):
@@ -221,22 +251,19 @@
         z1[c].wait_recv()
         b_v[pl.ds(depth + rank, rank), pl.ds(c * cw, cw)] = (-mm(answer_rows(1), st1[c])).astype(BF)
 
-    def third_far():
+    def third_far(j):
+        total = p2f[:, pl.ds(j * hw, hw)]
         for n in range(3):
-            x2[n].wait_recv()
-        for j in range(2):
-            lanes = pl.ds(j * hw, hw)
-            total = p2f[:, lanes]
-            for n in range(3):
-                total = total + p2_r[n, :, lanes].astype(F32)
-            st2[j, mine[2], :] = total.astype(BF)
-            f1[j] = share(st2.at[j, mine[2], :], far)
+            x2[n, j].wait_recv()
+            total = total + p2_r[n, j].astype(F32)
+        st2[j, mine[2], :] = total.astype(BF)
+        f1[j] = share(st2.at[j, mine[2], :], far)
 
     def third(j):
         f1[j].wait_recv()
         where = (pl.ds(depth + 2 * rank, rank), span(2 * spot + j, hw))
         b_v[where] = (-mm(answer_rows(2), st2[j])).astype(BF)
-        n2[j] = [share(b_v.at[where], to) for to in (diag, sib, near)]
+        n2[j] = [share(b_v.at[where], to) for to in team]
 
     def relay_piece(k):
         a_across[k].wait_recv()
@@ -250,26 +277,32 @@
             acc[other_rows, own] = mm(a_v[other_rows, pl.ds(0, early)], b_v[pl.ds(0, early), own])
 
     def finish(c, rows, start):
-        own = pl.ds(c * cw, cw)
+        own = span(c, cw)
         deep = pl.ds(start, depth + LEVELS * rank - start)
         out_v[rows, own] = (acc[rows, own] + mm(a_v[rows, deep], b_v[deep, own])).astype(BF)
 
-    second_sum(0)
-    second_sum(1)
     for l in range(2, 5):
         w_relay[l].wait_recv()
     first(0)
     first(1)
+    second_sum(0)
+    second_sum(1)
     relay_piece(0)
-    third_far()
+
+    @pl.when(inner == 1)
+    def _():
+        pl.semaphore_wait(msem, 1)
+
+    third_far(0)
+    third_far(1)
     relay_piece(1)
     second_sum(2)
     second(0)
     second_sum(3)
     second(1)
-    relay_piece(2)
     third(0)
     third(1)
+    relay_piece(2)
     first(2)
     first(3)
     for k in range(3):
@@ -278,14 +311,14 @@
     second(2)
     relay_piece(3)
     second(3)
-    for j in range(2):
-        for copy in n2[j]:
-            copy.wait_recv()
-    for c in range(CHUNKS):
-        finish(c, pair_rows, depth)
+    finish(spot, pair_rows, depth)
     relay[3].wait_recv()
-    for c in range(CHUNKS):
-        finish(c, other_rows, early)
+    finish(spot, other_rows, early)
+    for n in (2, 1, 0):
+        for j in range(2):
+            n2[j][n].wait_recv()
+        finish(spots[n], pair_rows, depth)
+        finish(spots[n], other_rows, early)
     for copy in copies:
         copy.wait_send()
 
@@ -319,13 +352,15 @@
             whole(F32),
             pltpu.VMEM((CHUNKS, 2 * rank, cw), BF),
             whole(F32), whole(BF), whole(BF),
-            pltpu.VMEM((rank, cw), F32), pltpu.VMEM((3, rank, cw), BF), pltpu.VMEM((3, rank, cw), BF),
+            pltpu.VMEM((rank, cw), F32), pltpu.VMEM((3, 2, rank, cw // 2), BF),
+            pltpu.VMEM((3, 2, rank, cw // 2), BF),
             pltpu.VMEM((CHUNKS, 2 * rank, cw), BF),
             pltpu.VMEM((2, 2 * rank, cw // 2), BF),
             pltpu.VMEM((rows, cols), F32),
             pltpu.SemaphoreType.DMA((11,)),
             pltpu.SemaphoreType.DMA((1,)),
-            pltpu.SemaphoreType.DMA((52,)),
+            pltpu.SemaphoreType.DMA((55,)),
+            pltpu.SemaphoreType.REGULAR,
         ],
         compiler_params=pltpu.CompilerParams(
             collective_id=0, has_side_effects=True, vmem_limit_bytes=40 * 1024 * 1024

time: 37 us -> 36.9 us (level)
  no operation moved by 1% of the time
where the time goes in v4:
time: 36.9 us; the launch traced here: 36.8 us
  Pallas kernels  35.5 us (96%)
  local copies, waits for them, and re-layouts  1.32 us (4%)
    pallas_call x1, Pallas kernels, local(): pl.pallas_call(kernel, out_shape=jax.ShapeDtypeStruct((rows, cols), BF),...  35.5 us
    unnamed x1, local copies, waits for them, and re-layouts  1.32 us

profile of v4, /device:TPU:0, one launch (start us, length us, event | category | flops | bytes accessed | tf_op | source)
XLA Modules:
  0.0 36.8 jit_solution(17836221565022179031)
XLA Ops:
  0.0 35.5 %shard_map.73 = bf16[1024,1024]{1,0:T(8,128)(2,1)S(1)} custom-call(bf16[1024,1024]{1,0:T(8,128)(2,1)} %b_hbm.1, bf16[256,1024]{1,0:T(8,128)(2,1)} %a_hbm.1, bf16[3,1024,128]{2,1,0:T(8,128)(2,1)} %p_hbm.1, bf16[3,1024,128]{2,1,0:T(8,128)(2,1)} %c_hbm.1, bf16[4,64,256]{2,1,0:T(8,128)(2,1)} %w0_hbm.1, bf16[2,64,256]{2,1,0:T(8,128)(2,1)} %w1_hbm.1, ...), custom_call_target="tpu_custom_call" | custom-call | tf_op jit(solution)/shard_map/pallas_call | solution.py:334
  35.5 1.3 %copy.9 = bf16[1024,1024]{1,0:T(8,128)(2,1)} copy(bf16[1024,1024]{1,0:T(8,128)(2,1)S(1)} %shard_map.73) | data formatting | bytes 4194304

commit v5 on v4

--- a/solution.py
+++ b/solution.py
@@ -31,7 +31,7 @@
 def kernel(
     b_hbm, a_hbm, p_hbm, c_hbm, w0_hbm, w1_hbm, w2_hbm, out_v,
     b_v, a_v, p_v, pt_v, w_v, g_v, gs_v, h_v, qf, q_s, q_r, q_v,
-    pf, st0, p1f, p1_s, p1_r, p2f, p2_s, p2_r, st1, st2, acc,
+    pf, st0, p1f, p1_s, p1_r, p2f, p2_s, p2_r, st1, st2, uf, u_s, u_r, acc,
     lsem, ssem, rsem, msem,
 ):
     i = lax.axis_index("leaf")
@@ -161,7 +161,7 @@
     def project(l, c):
         return pf[c] + mm(q_v[l, 1 - core], b_v[rest_cols, span(c, cw)])
 
-    x0, x1, x2 = {}, {}, {}
+    x0, x1, x2, z1, f1, n2, u1, relay = {}, {}, {}, {}, {}, {}, {}, {}
 
     def send0(c):
         x0[c] = share(st0.at[c, mine[0], :], sib)
@@ -172,8 +172,7 @@
     gather_q(0)
     for c in range(CHUNKS):
         st0[c, mine[0], :] = project(0, c).astype(BF)
-        if c < CHUNKS // 2:
-            send0(c)
+        send0(c)
 
     w_mate.wait_recv()
     g_send.wait_recv()
@@ -191,7 +190,8 @@
         p1f[c] = part
         p1_s[c] = part.astype(BF)
         if c < CHUNKS // 2:
-            send1(c)
+            st1[c, mine[1], :] = part.astype(BF)
+            z1[c] = send(p1_s.at[c], st1.at[c, mine[1], :], near)
 
     w_relay[1].wait_recv()
     gs_send.wait_recv()
@@ -226,8 +226,6 @@
     level_two(3)
     for c in range(CHUNKS // 2, CHUNKS):
         send1(c)
-    for c in range(CHUNKS // 2, CHUNKS):
-        send0(c)
     for l in range(3):
         w_late[l].wait_recv()
         lanes = span(1 - sides[l], rank) if l < 2 else pl.ds(0, 2 * rank)
@@ -236,7 +234,6 @@
     def answer_rows(l):
         return w_v[l, pl.ds(pl.multiple_of(sides[l] * 2, 2), 2), :, :].reshape(rank, 2 * rank)
 
-    z1, f1, n2, relay = {}, {}, {}, {}
 
     def first(c):
         x0[c].wait_recv()
@@ -250,6 +247,17 @@
     def second(c):
         z1[c].wait_recv()
         b_v[pl.ds(depth + rank, rank), pl.ds(c * cw, cw)] = (-mm(answer_rows(1), st1[c])).astype(BF)
+
+    def second_part(c):
+        z1[c].wait_recv()
+        part = mm(answer_rows(1), st1[c])
+        uf[c] = part
+        u_s[c] = part.astype(BF)
+        u1[c] = send(u_s.at[c], u_r.at[c], sib)
+
+    def second_join(c):
+        u1[c].wait_recv()
+        b_v[pl.ds(depth + rank, rank), pl.ds(c * cw, cw)] = (-(uf[c] + u_r[c].astype(F32))).astype(BF)
 
     def third_far(j):
         total = p2f[:, pl.ds(j * hw, hw)]
@@ -276,17 +284,23 @@
             own = pl.ds(c * cw, cw)
             acc[other_rows, own] = mm(a_v[other_rows, pl.ds(0, early)], b_v[pl.ds(0, early), own])
 
-    def finish(c, rows, start):
+    def add_last():
+        deep = pl.ds(early, piece)
+        for c in range(CHUNKS):
+            own = pl.ds(c * cw, cw)
+            acc[other_rows, own] = acc[other_rows, own] + mm(a_v[other_rows, deep], b_v[deep, own])
+
+    def finish(c):
         own = span(c, cw)
-        deep = pl.ds(start, depth + LEVELS * rank - start)
-        out_v[rows, own] = (acc[rows, own] + mm(a_v[rows, deep], b_v[deep, own])).astype(BF)
+        deep = pl.ds(depth, LEVELS * rank)
+        out_v[:, own] = (acc[:, own] + mm(a_v[:, deep], b_v[deep, own])).astype(BF)
 
     for l in range(2, 5):
         w_relay[l].wait_recv()
     first(0)
     first(1)
-    second_sum(0)
-    second_sum(1)
+    second_part(0)
+    second_part(1)
     relay_piece(0)
 
     @pl.when(inner == 1)
@@ -296,29 +310,29 @@
     third_far(0)
     third_far(1)
     relay_piece(1)
+    first(2)
+    first(3)
     second_sum(2)
-    second(0)
     second_sum(3)
-    second(1)
+    relay_piece(2)
     third(0)
     third(1)
-    relay_piece(2)
-    first(2)
-    first(3)
+    second_join(0)
+    second_join(1)
+    relay_piece(3)
     for k in range(3):
         relay[k].wait_recv()
     add_pieces()
     second(2)
-    relay_piece(3)
     second(3)
-    finish(spot, pair_rows, depth)
     relay[3].wait_recv()
-    finish(spot, other_rows, early)
+    add_last()
+    finish(spot)
     for n in (2, 1, 0):
         for j in range(2):
             n2[j][n].wait_recv()
-        finish(spots[n], pair_rows, depth)
-        finish(spots[n], other_rows, early)
+    for n in range(3):
+        finish(spots[n])
     for copy in copies:
         copy.wait_send()
 
@@ -356,6 +370,9 @@
             pltpu.VMEM((3, 2, rank, cw // 2), BF),
             pltpu.VMEM((CHUNKS, 2 * rank, cw), BF),
             pltpu.VMEM((2, 2 * rank, cw // 2), BF),
+            pltpu.VMEM((2, rank, cw), F32),
+            pltpu.VMEM((2, rank, cw), BF),
+            pltpu.VMEM((2, rank, cw), BF),
             pltpu.VMEM((rows, cols), F32),
             pltpu.SemaphoreType.DMA((11,)),
             pltpu.SemaphoreType.DMA((1,)),

time: 36.9 us -> 36.1 us (0.978)
  Pallas kernels: 35.5 us -> 34.6 us
    pallas_call x1, Pallas kernels: 35.5 us -> 34.6 us  [local(): pl.pallas_call(kernel, out_shape=jax.ShapeDtypeStruct((rows, cols), BF),...]
where the time goes in v5:
time: 36.1 us; the launch traced here: 35.9 us
  Pallas kernels  34.6 us (96%)
  local copies, waits for them, and re-layouts  1.32 us (4%)
    pallas_call x1, Pallas kernels, local(): pl.pallas_call(kernel, out_shape=jax.ShapeDtypeStruct((rows, cols), BF),...  34.6 us
    unnamed x1, local copies, waits for them, and re-layouts  1.32 us

profile of v5, /device:TPU:0, one launch (start us, length us, event | category | flops | bytes accessed | tf_op | source)
XLA Modules:
  0.0 35.9 jit_solution(920876039510320110)
XLA Ops:
  0.0 34.6 %shard_map.73 = bf16[1024,1024]{1,0:T(8,128)(2,1)S(1)} custom-call(bf16[1024,1024]{1,0:T(8,128)(2,1)} %b_hbm.1, bf16[256,1024]{1,0:T(8,128)(2,1)} %a_hbm.1, bf16[3,1024,128]{2,1,0:T(8,128)(2,1)} %p_hbm.1, bf16[3,1024,128]{2,1,0:T(8,128)(2,1)} %c_hbm.1, bf16[4,64,256]{2,1,0:T(8,128)(2,1)} %w0_hbm.1, bf16[2,64,256]{2,1,0:T(8,128)(2,1)} %w1_hbm.1, ...), custom_call_target="tpu_custom_call" | custom-call | tf_op jit(solution)/shard_map/pallas_call | solution.py:348
  34.6 1.3 %copy.9 = bf16[1024,1024]{1,0:T(8,128)(2,1)} copy(bf16[1024,1024]{1,0:T(8,128)(2,1)S(1)} %shard_map.73) | data formatting | bytes 4194304

commit v6 on v5

--- a/solution.py
+++ b/solution.py
@@ -8,6 +8,8 @@
 LEVELS = 3
 CHUNKS = 4
 PIECES = 4
+RECVS = 36
+FETCHES = 7
 BF = jnp.bfloat16
 F32 = jnp.float32
 
@@ -56,24 +58,33 @@
     chip = bit_of(r, 2)
 
     copies = []
-
-    def send(src, dst, to):
+    slots = {}
+
+    def slot(key):
+        return slots.setdefault(key, len(slots))
+
+    def send(src, dst, to, key):
         copy = pltpu.make_async_remote_copy(
-            src_ref=src, dst_ref=dst, send_sem=ssem.at[0], recv_sem=rsem.at[len(copies)],
+            src_ref=src, dst_ref=dst, send_sem=ssem.at[0], recv_sem=rsem.at[slot(key)],
             device_id=to, device_id_type=pl.DeviceIdType.MESH,
         )
         copy.start()
         copies.append(copy)
         return copy
 
-    def share(ref, to):
-        return send(ref, ref, to)
-
-    nloc = [0]
-
-    def fetch(src, dst):
-        copy = pltpu.make_async_copy(src, dst, lsem.at[nloc[0]])
-        nloc[0] += 1
+    def arrive(key, ref):
+        pltpu.make_async_copy(ref, ref, rsem.at[slot(key)]).wait()
+
+    def fetched(key, ref):
+        pltpu.make_async_copy(ref, ref, lsem.at[places[key]]).wait()
+
+    def share(ref, to, key):
+        return send(ref, ref, to, key)
+
+    places = {}
+
+    def fetch(src, dst, key):
+        copy = pltpu.make_async_copy(src, dst, lsem.at[places.setdefault(key, len(places))])
         copy.start()
         return copy
 
@@ -84,15 +95,15 @@
     half_cols = span(core, half)
     rest_cols = span(1 - core, half)
 
-    la = fetch(a_hbm, a_v.at[block, pl.ds(0, depth)])
-    lp = [fetch(p_hbm.at[0], p_v.at[:, pl.ds(0, rank)])]
-    lw = [
-        fetch(w_hbm.at[lax.div(i, 2 << level)], w_v.at[level, r])
+    la = fetch(a_hbm, a_v.at[block, pl.ds(0, depth)], "a")
+    lp = [fetch(p_hbm.at[0], p_v.at[:, pl.ds(0, rank)], "p0")]
+    [
+        fetch(w_hbm.at[lax.div(i, 2 << level)], w_v.at[level, r], "w")
         for level, w_hbm in enumerate((w0_hbm, w1_hbm, w2_hbm))
     ]
-    lp += [fetch(p_hbm.at[l], p_v.at[:, pl.ds(l * rank, rank)]) for l in range(1, LEVELS)]
-    lc = [fetch(c_hbm.at[l], a_v.at[:, pl.ds(depth + l * rank, rank)]) for l in range(LEVELS)]
-    lb = fetch(b_hbm, b_v.at[pl.ds(0, depth)])
+    lp += [fetch(p_hbm.at[l], p_v.at[:, pl.ds(l * rank, rank)], f"p{l}") for l in range(1, LEVELS)]
+    [fetch(c_hbm.at[l], a_v.at[:, pl.ds(depth + l * rank, rank)], "c") for l in range(LEVELS)]
+    lb = fetch(b_hbm, b_v.at[pl.ds(0, depth)], "b")
 
     barrier = pltpu.get_barrier_semaphore()
     inner = lax.rem(sides[1] + sides[2], 2)
@@ -111,10 +122,9 @@
         pl.semaphore_signal(msem, inc=1, device_id=mid, device_id_type=pl.DeviceIdType.MESH)
 
 
-    a_mate = share(a_v.at[block, rest_cols], mate)
-    for copy in lw:
-        copy.wait()
-    w_early = [share(w_v.at[l, r, :, mine[l]], across) for l in range(2)]
+    a_mate = share(a_v.at[block, rest_cols], mate, "am")
+    fetched("w", w_v.at[:, r])
+    [share(w_v.at[l, r, :, mine[l]], across, "we") for l in range(2)]
     lp[0].wait()
     pt_v[0] = p_v[:, pl.ds(0, rank)].T
     a_mate.wait_recv()
@@ -126,24 +136,22 @@
         part = mm(pt_v[l, :, pair_rows], a_v[pair_rows, half_cols])
         qf[l] = part
         q_s[l] = part.astype(BF)
-        q_across.append(send(q_s.at[l], q_r.at[l], across))
-    a_mate2 = share(a_v.at[block, half_cols], mate)
-    w_mate = share(w_v.at[:, r], mate)
-    w_late = [share(w_v.at[l, r, :, span(1 - sides[l], rank)], across) for l in range(2)]
-    w_late.append(share(w_v.at[2, r], across))
-    a_across = [share(a_v.at[block, pl.ds(k * piece, piece)], across) for k in range(PIECES)]
-
-    for copy in lc:
-        copy.wait()
+        q_across.append(send(q_s.at[l], q_r.at[l], across, f"q{l}"))
+    a_mate2 = share(a_v.at[block, half_cols], mate, "an")
+    w_mate = share(w_v.at[:, r], mate, "wm")
+    [share(w_v.at[l, r, :, span(1 - sides[l], rank)], across, "wl") for l in range(2)]
+    share(w_v.at[2, r], across, "wl")
+    a_across = [share(a_v.at[block, pl.ds(k * piece, piece)], across, f"a{k}") for k in range(PIECES)]
+
+    fetched("c", a_v.at[:, pl.ds(depth, LEVELS * rank)])
     for n, (l, k) in enumerate(((1, 0), (2, 0), (2, 1))):
         g_v[n, :, mine[0]] = mm(pt_v[l], a_v[:, pl.ds(depth + k * rank, rank)]).astype(BF)
-    g_send = share(g_v.at[:, :, mine[0]], sib)
+    g_send = share(g_v.at[:, :, mine[0]], sib, "g")
 
     over = flip(r, 2)
-    w_relay = []
+    arrive("we", w_v.at[0, r])
     for l in range(2):
-        w_early[l].wait_recv()
-        w_relay.append(share(w_v.at[l, over, :, mine[l]], mate))
+        share(w_v.at[l, over, :, mine[l]], mate, "re")
     lb.wait()
     a_mate2.wait_recv()
     for c in range(CHUNKS):
@@ -153,7 +161,7 @@
     def gather_q(l):
         q_across[l].wait_recv()
         q_v[l, core] = (qf[l] + q_r[l].astype(F32)).astype(BF)
-        relayed = share(q_v.at[l, core], mate)
+        relayed = share(q_v.at[l, core], mate, f"m{l}")
         for c in range(CHUNKS):
             pf[c] = mm(q_v[l, core], b_v[half_cols, pl.ds(c * cw, cw)])
         relayed.wait_recv()
@@ -161,13 +169,13 @@
     def project(l, c):
         return pf[c] + mm(q_v[l, 1 - core], b_v[rest_cols, span(c, cw)])
 
-    x0, x1, x2, z1, f1, n2, u1, relay = {}, {}, {}, {}, {}, {}, {}, {}
+    x1, z1, f1, u1, relay = {}, {}, {}, {}, {}
 
     def send0(c):
-        x0[c] = share(st0.at[c, mine[0], :], sib)
+        share(st0.at[c, mine[0], :], sib, f"x{c // 2}")
 
     def send1(c):
-        x1[c] = send(p1_s.at[c], p1_r.at[c], sib)
+        x1[c] = send(p1_s.at[c], p1_r.at[c], sib, f"y{c}")
 
     gather_q(0)
     for c in range(CHUNKS):
@@ -176,13 +184,13 @@
 
     w_mate.wait_recv()
     g_send.wait_recv()
-    w_relay[0].wait_recv()
+    arrive("re", w_v.at[0, r])
     w_cols = w_v[0, :, :, mine[0]].reshape(2 * rank, rank)
     for n in range(2):
         h_v[n] = mm(g_v[n], w_cols).astype(BF)
     pair_sum = g_v[2, :, pl.ds(0, rank)].astype(F32) + g_v[2, :, pl.ds(rank, rank)].astype(F32)
     gs_v[:, mine[1]] = pair_sum.astype(BF)
-    gs_send = share(gs_v.at[:, mine[1]], near)
+    gs_send = share(gs_v.at[:, mine[1]], near, "gs")
 
     gather_q(1)
     for c in range(CHUNKS):
@@ -191,9 +199,8 @@
         p1_s[c] = part.astype(BF)
         if c < CHUNKS // 2:
             st1[c, mine[1], :] = part.astype(BF)
-            z1[c] = send(p1_s.at[c], st1.at[c, mine[1], :], near)
-
-    w_relay[1].wait_recv()
+            z1[c] = send(p1_s.at[c], st1.at[c, mine[1], :], near, f"z{c}")
+
     gs_send.wait_recv()
     h_v[2] = mm(gs_v[...], w_v[1, :, :, mine[1]].reshape(2 * rank, rank)).astype(BF)
 
@@ -209,10 +216,10 @@
             p2f[...] = part
         else:
             for h in range(2):
-                p2_s[n, h] = part[:, h * hw:(h + 1) * hw].astype(BF)
+                p2_s[h, n] = part[:, h * hw:(h + 1) * hw].astype(BF)
 
     def send2(n, h):
-        x2[n, h] = send(p2_s.at[n, h], p2_r.at[n, h], team[n])
+        send(p2_s.at[h, n], p2_r.at[h, n], team[n], f"t{h}")
 
     level_two(0)
     send2(0, 0)
@@ -226,23 +233,24 @@
     level_two(3)
     for c in range(CHUNKS // 2, CHUNKS):
         send1(c)
+    arrive("wl", w_v.at[pl.ds(0, 2), r])
     for l in range(3):
-        w_late[l].wait_recv()
         lanes = span(1 - sides[l], rank) if l < 2 else pl.ds(0, 2 * rank)
-        w_relay.append(share(w_v.at[l, over, :, lanes], mate))
+        share(w_v.at[l, over, :, lanes], mate, "rl")
 
     def answer_rows(l):
         return w_v[l, pl.ds(pl.multiple_of(sides[l] * 2, 2), 2), :, :].reshape(rank, 2 * rank)
 
 
-    def first(c):
-        x0[c].wait_recv()
-        b_v[pl.ds(depth, rank), pl.ds(c * cw, cw)] = (-mm(answer_rows(0), st0[c])).astype(BF)
+    def first(pair):
+        arrive(f"x{pair[0] // 2}", st0.at[pl.ds(pair[0], 2), mine[0], :])
+        for c in pair:
+            b_v[pl.ds(depth, rank), pl.ds(c * cw, cw)] = (-mm(answer_rows(0), st0[c])).astype(BF)
 
     def second_sum(c):
         x1[c].wait_recv()
         st1[c, mine[1], :] = (p1f[c] + p1_r[c].astype(F32)).astype(BF)
-        z1[c] = share(st1.at[c, mine[1], :], near)
+        z1[c] = share(st1.at[c, mine[1], :], near, f"z{c}")
 
     def second(c):
         z1[c].wait_recv()
@@ -253,7 +261,7 @@
         part = mm(answer_rows(1), st1[c])
         uf[c] = part
         u_s[c] = part.astype(BF)
-        u1[c] = send(u_s.at[c], u_r.at[c], sib)
+        u1[c] = send(u_s.at[c], u_r.at[c], sib, f"u{c}")
 
     def second_join(c):
         u1[c].wait_recv()
@@ -261,21 +269,22 @@
 
     def third_far(j):
         total = p2f[:, pl.ds(j * hw, hw)]
+        arrive(f"t{j}", p2_r.at[j])
         for n in range(3):
-            x2[n, j].wait_recv()
-            total = total + p2_r[n, j].astype(F32)
+            total = total + p2_r[j, n].astype(F32)
         st2[j, mine[2], :] = total.astype(BF)
-        f1[j] = share(st2.at[j, mine[2], :], far)
+        f1[j] = share(st2.at[j, mine[2], :], far, f"f{j}")
 
     def third(j):
         f1[j].wait_recv()
         where = (pl.ds(depth + 2 * rank, rank), span(2 * spot + j, hw))
         b_v[where] = (-mm(answer_rows(2), st2[j])).astype(BF)
-        n2[j] = [share(b_v.at[where], to) for to in team]
+        for to in team:
+            share(b_v.at[where], to, "n")
 
     def relay_piece(k):
         a_across[k].wait_recv()
-        relay[k] = share(a_v.at[span(over, blk), pl.ds(k * piece, piece)], mate)
+        relay[k] = share(a_v.at[span(over, blk), pl.ds(k * piece, piece)], mate, "r3" if k == PIECES - 1 else "r")
 
     early = depth - piece
 
@@ -291,14 +300,12 @@
             acc[other_rows, own] = acc[other_rows, own] + mm(a_v[other_rows, deep], b_v[deep, own])
 
     def finish(c):
-        own = span(c, cw)
+        own = pl.ds(c * cw, cw)
         deep = pl.ds(depth, LEVELS * rank)
         out_v[:, own] = (acc[:, own] + mm(a_v[:, deep], b_v[deep, own])).astype(BF)
 
-    for l in range(2, 5):
-        w_relay[l].wait_recv()
-    first(0)
-    first(1)
+    arrive("rl", w_v.at[pl.ds(0, 2), r])
+    first((0, 1))
     second_part(0)
     second_part(1)
     relay_piece(0)
@@ -310,8 +317,7 @@
     third_far(0)
     third_far(1)
     relay_piece(1)
-    first(2)
-    first(3)
+    first((2, 3))
     second_sum(2)
     second_sum(3)
     relay_piece(2)
@@ -320,19 +326,16 @@
     second_join(0)
     second_join(1)
     relay_piece(3)
-    for k in range(3):
-        relay[k].wait_recv()
+    arrive("r", a_v.at[block, pl.ds(0, early)])
     add_pieces()
     second(2)
     second(3)
     relay[3].wait_recv()
     add_last()
-    finish(spot)
-    for n in (2, 1, 0):
-        for j in range(2):
-            n2[j][n].wait_recv()
-    for n in range(3):
-        finish(spots[n])
+    arrive("n", b_v.at[pl.ds(depth + 2 * rank, rank), pl.ds(0, (CHUNKS - 1) * cw)])
+    for c in range(CHUNKS):
+        finish(c)
+    assert len(slots) == RECVS and len(places) == FETCHES, (len(slots), len(places))
     for copy in copies:
         copy.wait_send()
 
@@ -366,17 +369,17 @@
             whole(F32),
             pltpu.VMEM((CHUNKS, 2 * rank, cw), BF),
             whole(F32), whole(BF), whole(BF),
-            pltpu.VMEM((rank, cw), F32), pltpu.VMEM((3, 2, rank, cw // 2), BF),
-            pltpu.VMEM((3, 2, rank, cw // 2), BF),
+            pltpu.VMEM((rank, cw), F32), pltpu.VMEM((2, 3, rank, cw // 2), BF),
+            pltpu.VMEM((2, 3, rank, cw // 2), BF),
             pltpu.VMEM((CHUNKS, 2 * rank, cw), BF),
             pltpu.VMEM((2, 2 * rank, cw // 2), BF),
             pltpu.VMEM((2, rank, cw), F32),
             pltpu.VMEM((2, rank, cw), BF),
             pltpu.VMEM((2, rank, cw), BF),
             pltpu.VMEM((rows, cols), F32),
-            pltpu.SemaphoreType.DMA((11,)),
+            pltpu.SemaphoreType.DMA((FETCHES,)),
             pltpu.SemaphoreType.DMA((1,)),
-            pltpu.SemaphoreType.DMA((55,)),
+            pltpu.SemaphoreType.DMA((RECVS,)),
             pltpu.SemaphoreType.REGULAR,
         ],
         compiler_params=pltpu.CompilerParams(

time: 36.1 us -> 35.7 us (0.989)
  Pallas kernels: 34.6 us -> 34.2 us
    pallas_call x1, Pallas kernels: 34.6 us -> 34.2 us  [local(): pl.pallas_call(kernel, out_shape=jax.ShapeDtypeStruct((rows, cols), BF),...]
where the time goes in v6:
time: 35.7 us; the launch traced here: 35.5 us
  Pallas kernels  34.2 us (96%)
  local copies, waits for them, and re-layouts  1.32 us (4%)
    pallas_call x1, Pallas kernels, local(): pl.pallas_call(kernel, out_shape=jax.ShapeDtypeStruct((rows, cols), BF),...  34.2 us
    unnamed x1, local copies, waits for them, and re-layouts  1.32 us

profile of v6, /device:TPU:0, one launch (start us, length us, event | category | flops | bytes accessed | tf_op | source)
XLA Modules:
  0.0 35.5 jit_solution(11265227378596769150)
XLA Ops:
  0.0 34.2 %shard_map.73 = bf16[1024,1024]{1,0:T(8,128)(2,1)S(1)} custom-call(bf16[1024,1024]{1,0:T(8,128)(2,1)} %b_hbm.1, bf16[256,1024]{1,0:T(8,128)(2,1)} %a_hbm.1, bf16[3,1024,128]{2,1,0:T(8,128)(2,1)} %p_hbm.1, bf16[3,1024,128]{2,1,0:T(8,128)(2,1)} %c_hbm.1, bf16[4,64,256]{2,1,0:T(8,128)(2,1)} %w0_hbm.1, bf16[2,64,256]{2,1,0:T(8,128)(2,1)} %w1_hbm.1, ...), custom_call_target="tpu_custom_call" | custom-call | tf_op jit(solution)/shard_map/pallas_call | solution.py:351
  34.2 1.3 %copy.9 = bf16[1024,1024]{1,0:T(8,128)(2,1)} copy(bf16[1024,1024]{1,0:T(8,128)(2,1)S(1)} %shard_map.73) | data formatting | bytes 4194304

commit v7 on v6

--- a/solution.py
+++ b/solution.py
@@ -8,6 +8,7 @@
 LEVELS = 3
 CHUNKS = 4
 PIECES = 4
+ZFIRST = 3
 RECVS = 36
 FETCHES = 7
 BF = jnp.bfloat16
@@ -192,14 +193,18 @@
     gs_v[:, mine[1]] = pair_sum.astype(BF)
     gs_send = share(gs_v.at[:, mine[1]], near, "gs")
 
+    def cross(c):
+        z1[c] = send(p1_s.at[c], st1.at[c, mine[1], :], near, f"z{c}")
+
     gather_q(1)
     for c in range(CHUNKS):
         part = project(1, c) - mm(h_v[0], st0[c, mine[0], :])
         p1f[c] = part
         p1_s[c] = part.astype(BF)
-        if c < CHUNKS // 2:
+        if c < ZFIRST:
             st1[c, mine[1], :] = part.astype(BF)
-            z1[c] = send(p1_s.at[c], st1.at[c, mine[1], :], near, f"z{c}")
+        if c < 2:
+            cross(c)
 
     gs_send.wait_recv()
     h_v[2] = mm(gs_v[...], w_v[1, :, :, mine[1]].reshape(2 * rank, rank)).astype(BF)
@@ -231,8 +236,8 @@
     send2(2, 0)
     send2(2, 1)
     level_two(3)
-    for c in range(CHUNKS // 2, CHUNKS):
-        send1(c)
+    cross(2)
+    send1(3)
     arrive("wl", w_v.at[pl.ds(0, 2), r])
     for l in range(3):
         lanes = span(1 - sides[l], rank) if l < 2 else pl.ds(0, 2 * rank)
@@ -318,8 +323,8 @@
     third_far(1)
     relay_piece(1)
     first((2, 3))
-    second_sum(2)
     second_sum(3)
+    second_part(2)
     relay_piece(2)
     third(0)
     third(1)
@@ -328,8 +333,8 @@
     relay_piece(3)
     arrive("r", a_v.at[block, pl.ds(0, early)])
     add_pieces()
-    second(2)
     second(3)
+    second_join(2)
     relay[3].wait_recv()
     add_last()
     arrive("n", b_v.at[pl.ds(depth + 2 * rank, rank), pl.ds(0, (CHUNKS - 1) * cw)])
@@ -373,9 +378,9 @@
             pltpu.VMEM((2, 3, rank, cw // 2), BF),
             pltpu.VMEM((CHUNKS, 2 * rank, cw), BF),
             pltpu.VMEM((2, 2 * rank, cw // 2), BF),
-            pltpu.VMEM((2, rank, cw), F32),
-            pltpu.VMEM((2, rank, cw), BF),
-            pltpu.VMEM((2, rank, cw), BF),
+            pltpu.VMEM((ZFIRST, rank, cw), F32),
+            pltpu.VMEM((ZFIRST, rank, cw), BF),
+            pltpu.VMEM((ZFIRST, rank, cw), BF),
             pltpu.VMEM((rows, cols), F32),
             pltpu.SemaphoreType.DMA((FETCHES,)),
             pltpu.SemaphoreType.DMA((1,)),

time: 35.7 us -> 34.7 us (0.972)
  Pallas kernels: 34.2 us -> 33.2 us
    pallas_call x1, Pallas kernels: 34.2 us -> 33.2 us  [local(): pl.pallas_call(kernel, out_shape=jax.ShapeDtypeStruct((rows, cols), BF),...]
where the time goes in v7:
time: 34.7 us; the launch traced here: 34.6 us
  Pallas kernels  33.2 us (96%)
  local copies, waits for them, and re-layouts  1.32 us (4%)
    pallas_call x1, Pallas kernels, local(): pl.pallas_call(kernel, out_shape=jax.ShapeDtypeStruct((rows, cols), BF),...  33.2 us
    unnamed x1, local copies, waits for them, and re-layouts  1.32 us

profile of v7, /device:TPU:0, one launch (start us, length us, event | category | flops | bytes accessed | tf_op | source)
XLA Modules:
  0.0 34.6 jit_solution(9195726137340581087)
XLA Ops:
  0.0 33.2 %shard_map.73 = bf16[1024,1024]{1,0:T(8,128)(2,1)S(1)} custom-call(bf16[1024,1024]{1,0:T(8,128)(2,1)} %b_hbm.1, bf16[256,1024]{1,0:T(8,128)(2,1)} %a_hbm.1, bf16[3,1024,128]{2,1,0:T(8,128)(2,1)} %p_hbm.1, bf16[3,1024,128]{2,1,0:T(8,128)(2,1)} %c_hbm.1, bf16[4,64,256]{2,1,0:T(8,128)(2,1)} %w0_hbm.1, bf16[2,64,256]{2,1,0:T(8,128)(2,1)} %w1_hbm.1, ...), custom_call_target="tpu_custom_call" | custom-call | tf_op jit(solution)/shard_map/pallas_call | solution.py:356
  33.2 1.3 %copy.9 = bf16[1024,1024]{1,0:T(8,128)(2,1)} copy(bf16[1024,1024]{1,0:T(8,128)(2,1)S(1)} %shard_map.73) | data formatting | bytes 4194304

commit v8 on v7

--- a/solution.py
+++ b/solution.py
@@ -9,7 +9,7 @@
 CHUNKS = 4
 PIECES = 4
 ZFIRST = 3
-RECVS = 36
+RECVS = 41
 FETCHES = 7
 BF = jnp.bfloat16
 F32 = jnp.float32
@@ -34,7 +34,7 @@
 def kernel(
     b_hbm, a_hbm, p_hbm, c_hbm, w0_hbm, w1_hbm, w2_hbm, out_v,
     b_v, a_v, p_v, pt_v, w_v, g_v, gs_v, h_v, qf, q_s, q_r, q_v,
-    pf, st0, p1f, p1_s, p1_r, p2f, p2_s, p2_r, st1, st2, uf, u_s, u_r, acc,
+    pf, st0, p1f, p1_s, p1_r, p2f, p2_s, p2_r, st1, st2, a2_s, uf, u_s, u_r, acc,
     lsem, ssem, rsem, msem,
 ):
     i = lax.axis_index("leaf")
@@ -52,7 +52,6 @@
     sib = {"leaf": flip(i, 1)}
     near = {"leaf": flip(i, 2)}
     far = {"leaf": flip(i, 4)}
-    diag = {"leaf": flip(flip(i, 1), 2)}
     mid = {"leaf": flip(flip(i, 2), 4)}
     sides = [bit_of(i, 1), bit_of(i, 2), bit_of(i, 4)]
     core = bit_of(r, 1)
@@ -64,13 +63,15 @@
     def slot(key):
         return slots.setdefault(key, len(slots))
 
-    def send(src, dst, to, key):
+    def send(src, dst, to, key, extra=None, keep=True):
+        place = slot(key) if extra is None else slot(key) + extra
         copy = pltpu.make_async_remote_copy(
-            src_ref=src, dst_ref=dst, send_sem=ssem.at[0], recv_sem=rsem.at[slot(key)],
+            src_ref=src, dst_ref=dst, send_sem=ssem.at[0], recv_sem=rsem.at[place],
             device_id=to, device_id_type=pl.DeviceIdType.MESH,
         )
         copy.start()
-        copies.append(copy)
+        if keep:
+            copies.append(copy)
         return copy
 
     def arrive(key, ref):
@@ -212,19 +213,21 @@
     gather_q(2)
     spot = 2 * sides[1] + sides[0]
     spots = (3 - spot, flip(spot, 1), flip(spot, 2), spot)
-    team = (diag, sib, near)
+    leaves = (flip(flip(i, 1), 2), flip(i, 1), flip(i, 2))
+    odd_team = [{"leaf": leaf, "rhs": 2 * chip + 1} for leaf in leaves]
+    odd_keys = [[slot(f"t{w}{h}") for h in range(2)] for w in range(2)]
 
     def level_two(n):
         who = spots[n]
         part = project(2, who) - mm(h_v[1], st0[who, mine[0], :]) - mm(h_v[2], p1_s[who])
         if n == 3:
-            p2f[...] = part
+            p2f[core] = part
         else:
             for h in range(2):
                 p2_s[h, n] = part[:, h * hw:(h + 1) * hw].astype(BF)
 
     def send2(n, h):
-        send(p2_s.at[h, n], p2_r.at[h, n], team[n], f"t{h}")
+        send(p2_s.at[h, n], p2_r.at[core, h, n], odd_team[n], f"t0{h}", extra=2 * core)
 
     level_two(0)
     send2(0, 0)
@@ -236,6 +239,11 @@
     send2(2, 0)
     send2(2, 1)
     level_two(3)
+
+    @pl.when(core == 0)
+    def _():
+        send(p2f.at[0], p2f.at[0], mate, "tf", keep=False)
+
     cross(2)
     send1(3)
     arrive("wl", w_v.at[pl.ds(0, 2), r])
@@ -272,20 +280,30 @@
         u1[c].wait_recv()
         b_v[pl.ds(depth + rank, rank), pl.ds(c * cw, cw)] = (-(uf[c] + u_r[c].astype(F32))).astype(BF)
 
-    def third_far(j):
-        total = p2f[:, pl.ds(j * hw, hw)]
-        arrive(f"t{j}", p2_r.at[j])
+    where = [(pl.ds(depth + 2 * rank, rank), span(2 * spot + j, hw)) for j in range(2)]
+    same_team = [{"leaf": leaf} for leaf in leaves]
+    even_team = [{"leaf": leaf, "rhs": flip(r, 1)} for leaf in leaves] + [mate]
+
+    def third_far(w, j):
+        total = p2f[w, :, pl.ds(j * hw, hw)]
+        arrive(f"t{w}{j}", p2_r.at[w, j])
         for n in range(3):
-            total = total + p2_r[j, n].astype(F32)
-        st2[j, mine[2], :] = total.astype(BF)
-        f1[j] = share(st2.at[j, mine[2], :], far, f"f{j}")
-
-    def third(j):
-        f1[j].wait_recv()
-        where = (pl.ds(depth + 2 * rank, rank), span(2 * spot + j, hw))
-        b_v[where] = (-mm(answer_rows(2), st2[j])).astype(BF)
-        for to in team:
-            share(b_v.at[where], to, "n")
+            total = total + p2_r[w, j, n].astype(F32)
+        st2[w, j, mine[2], :] = total.astype(BF)
+        ours = st2.at[w, j, mine[2], :]
+        send(ours, ours, far, f"f{w}{j}", keep=False)
+
+    def third(w, j):
+        arrive(f"f{w}{j}", st2.at[w, j, mine[2], :])
+        value = (-mm(answer_rows(2), st2[w, j])).astype(BF)
+        if w == 1:
+            b_v[where[j]] = value
+            for to in same_team:
+                send(b_v.at[where[j]], b_v.at[where[j]], to, "n", keep=False)
+        else:
+            a2_s[j] = value
+            for to in even_team:
+                send(a2_s.at[j], b_v.at[where[j]], to, "n", keep=False)
 
     def relay_piece(k):
         a_across[k].wait_recv()
@@ -319,15 +337,25 @@
     def _():
         pl.semaphore_wait(msem, 1)
 
-    third_far(0)
-    third_far(1)
+    @pl.when(core == 1)
+    def _():
+        arrive("tf", p2f.at[0])
+        for j in range(2):
+            third_far(1, j)
+            third_far(0, j)
+
     relay_piece(1)
     first((2, 3))
     second_sum(3)
     second_part(2)
     relay_piece(2)
-    third(0)
-    third(1)
+
+    @pl.when(core == 1)
+    def _():
+        for j in range(2):
+            third(1, j)
+            third(0, j)
+
     second_join(0)
     second_join(1)
     relay_piece(3)
@@ -337,12 +365,34 @@
     second_join(2)
     relay[3].wait_recv()
     add_last()
-    arrive("n", b_v.at[pl.ds(depth + 2 * rank, rank), pl.ds(0, (CHUNKS - 1) * cw)])
+    answers = pl.ds(depth + 2 * rank, rank)
+
+    @pl.when(core == 1)
+    def _():
+        arrive("n", b_v.at[answers, pl.ds(0, (CHUNKS - 1) * cw)])
+
+    @pl.when(core == 0)
+    def _():
+        arrive("n", b_v.at[answers, pl.ds(0, CHUNKS * cw)])
+
     for c in range(CHUNKS):
         finish(c)
     assert len(slots) == RECVS and len(places) == FETCHES, (len(slots), len(places))
     for copy in copies:
         copy.wait_send()
+
+    def sent(ref):
+        pltpu.make_async_copy(ref, ref, ssem.at[0]).wait()
+
+    @pl.when(core == 1)
+    def _():
+        for w in range(2):
+            sent(b_v.at[answers, pl.ds(0, CHUNKS * cw)])
+        sent(st2.at[0, 0])
+
+    @pl.when(core == 0)
+    def _():
+        sent(p2f.at[0])
 
 
 def local(right_sides, leaf_inverse, project_factors, correct_factors, *couplings):
@@ -374,10 +424,11 @@
             whole(F32),
             pltpu.VMEM((CHUNKS, 2 * rank, cw), BF),
             whole(F32), whole(BF), whole(BF),
-            pltpu.VMEM((rank, cw), F32), pltpu.VMEM((2, 3, rank, cw // 2), BF),
-            pltpu.VMEM((2, 3, rank, cw // 2), BF),
+            pltpu.VMEM((2, rank, cw), F32), pltpu.VMEM((2, 3, rank, cw // 2), BF),
+            pltpu.VMEM((2, 2, 3, rank, cw // 2), BF),
             pltpu.VMEM((CHUNKS, 2 * rank, cw), BF),
-            pltpu.VMEM((2, 2 * rank, cw // 2), BF),
+            pltpu.VMEM((2, 2, 2 * rank, cw // 2), BF),
+            pltpu.VMEM((2, rank, cw // 2), BF),
             pltpu.VMEM((ZFIRST, rank, cw), F32),
             pltpu.VMEM((ZFIRST, rank, cw), BF),
             pltpu.VMEM((ZFIRST, rank, cw), BF),

time: 34.7 us -> 34.8 us (level)
  no operation moved by 1% of the time
where the time goes in v8:
time: 34.8 us; the launch traced here: 34.6 us
  Pallas kernels  33.3 us (96%)
  local copies, waits for them, and re-layouts  1.32 us (4%)
    pallas_call x1, Pallas kernels, local(): pl.pallas_call(kernel, out_shape=jax.ShapeDtypeStruct((rows, cols), BF),...  33.3 us
    unnamed x1, local copies, waits for them, and re-layouts  1.32 us

profile of v8, /device:TPU:0, one launch (start us, length us, event | category | flops | bytes accessed | tf_op | source)
XLA Modules:
  0.0 34.6 jit_solution(10693001158706094004)
XLA Ops:
  0.0 33.3 %shard_map.73 = bf16[1024,1024]{1,0:T(8,128)(2,1)S(1)} custom-call(bf16[1024,1024]{1,0:T(8,128)(2,1)} %b_hbm.1, bf16[256,1024]{1,0:T(8,128)(2,1)} %a_hbm.1, bf16[3,1024,128]{2,1,0:T(8,128)(2,1)} %p_hbm.1, bf16[3,1024,128]{2,1,0:T(8,128)(2,1)} %c_hbm.1, bf16[4,64,256]{2,1,0:T(8,128)(2,1)} %w0_hbm.1, bf16[2,64,256]{2,1,0:T(8,128)(2,1)} %w1_hbm.1, ...), custom_call_target="tpu_custom_call" | custom-call | tf_op jit(solution)/shard_map/pallas_call | solution.py:406
  33.3 1.3 %copy.9 = bf16[1024,1024]{1,0:T(8,128)(2,1)} copy(bf16[1024,1024]{1,0:T(8,128)(2,1)S(1)} %shard_map.73) | data formatting | bytes 4194304

commit v9 on v8

--- a/solution.py
+++ b/solution.py
@@ -7,9 +7,10 @@
 
 LEVELS = 3
 CHUNKS = 4
-PIECES = 4
+SPLIT = ((0, 1), (1, 2), (3, 2), (5, 2), (7, 1))
+UNITS = 8
 ZFIRST = 3
-RECVS = 41
+RECVS = 43
 FETCHES = 7
 BF = jnp.bfloat16
 F32 = jnp.float32
@@ -34,7 +35,7 @@
 def kernel(
     b_hbm, a_hbm, p_hbm, c_hbm, w0_hbm, w1_hbm, w2_hbm, out_v,
     b_v, a_v, p_v, pt_v, w_v, g_v, gs_v, h_v, qf, q_s, q_r, q_v,
-    pf, st0, p1f, p1_s, p1_r, p2f, p2_s, p2_r, st1, st2, a2_s, uf, u_s, u_r, acc,
+    pf, st0, p1f, p1_s, p1_r, p2f, p2_s, p2o, p2_r, st1, st2, a2_s, uf, u_s, u_r, acc,
     lsem, ssem, rsem, msem,
 ):
     i = lax.axis_index("leaf")
@@ -46,7 +47,9 @@
     cw = cols // CHUNKS
     hw = cw // 2
     half = depth // 2
-    piece = depth // PIECES
+    unit = depth // UNITS
+    pieces = [pl.ds(at * unit, size * unit) for at, size in SPLIT]
+    final = len(SPLIT) - 1
     mate = {"rhs": flip(r, 1)}
     across = {"rhs": flip(r, 2)}
     sib = {"leaf": flip(i, 1)}
@@ -125,6 +128,7 @@
 
 
     a_mate = share(a_v.at[block, rest_cols], mate, "am")
+    a_across = [share(a_v.at[block, pieces[0]], across, "a0")]
     fetched("w", w_v.at[:, r])
     [share(w_v.at[l, r, :, mine[l]], across, "we") for l in range(2)]
     lp[0].wait()
@@ -143,7 +147,8 @@
     w_mate = share(w_v.at[:, r], mate, "wm")
     [share(w_v.at[l, r, :, span(1 - sides[l], rank)], across, "wl") for l in range(2)]
     share(w_v.at[2, r], across, "wl")
-    a_across = [share(a_v.at[block, pl.ds(k * piece, piece)], across, f"a{k}") for k in range(PIECES)]
+    for k in range(1, len(SPLIT)):
+        a_across.append(share(a_v.at[block, pieces[k]], across, f"a{k}"))
 
     fetched("c", a_v.at[:, pl.ds(depth, LEVELS * rank)])
     for n, (l, k) in enumerate(((1, 0), (2, 0), (2, 1))):
@@ -217,32 +222,21 @@
     odd_team = [{"leaf": leaf, "rhs": 2 * chip + 1} for leaf in leaves]
     odd_keys = [[slot(f"t{w}{h}") for h in range(2)] for w in range(2)]
 
-    def level_two(n):
-        who = spots[n]
-        part = project(2, who) - mm(h_v[1], st0[who, mine[0], :]) - mm(h_v[2], p1_s[who])
-        if n == 3:
-            p2f[core] = part
-        else:
-            for h in range(2):
-                p2_s[h, n] = part[:, h * hw:(h + 1) * hw].astype(BF)
-
-    def send2(n, h):
-        send(p2_s.at[h, n], p2_r.at[core, h, n], odd_team[n], f"t0{h}", extra=2 * core)
-
-    level_two(0)
-    send2(0, 0)
-    level_two(1)
-    send2(1, 0)
-    send2(0, 1)
-    send2(1, 1)
-    level_two(2)
-    send2(2, 0)
-    send2(2, 1)
-    level_two(3)
+    def part_of(who, h):
+        return 2 * h + lax.div(who, 2), slice(None), span(lax.rem(who, 2), hw)
+
+    for h in range(2):
+        for c in (2 * h, 2 * h + 1):
+            part = project(2, c) - mm(h_v[1], st0[c, mine[0], :]) - mm(h_v[2], p1_s[c])
+            p2f[c] = part
+            p2_s[c] = part.astype(BF)
+        for n in range(3):
+            send(p2_s.at[part_of(spots[n], h)], p2_r.at[core, h, n], odd_team[n], f"t0{h}", extra=2 * core)
+        p2o[core, h] = p2f[part_of(spot, h)]
 
     @pl.when(core == 0)
     def _():
-        send(p2f.at[0], p2f.at[0], mate, "tf", keep=False)
+        send(p2o.at[0], p2o.at[0], mate, "tf", keep=False)
 
     cross(2)
     send1(3)
@@ -280,12 +274,12 @@
         u1[c].wait_recv()
         b_v[pl.ds(depth + rank, rank), pl.ds(c * cw, cw)] = (-(uf[c] + u_r[c].astype(F32))).astype(BF)
 
-    where = [(pl.ds(depth + 2 * rank, rank), span(2 * spot + j, hw)) for j in range(2)]
+    where = [(pl.ds(depth + 2 * rank, rank), span(4 * j + spot, hw)) for j in range(2)]
     same_team = [{"leaf": leaf} for leaf in leaves]
     even_team = [{"leaf": leaf, "rhs": flip(r, 1)} for leaf in leaves] + [mate]
 
     def third_far(w, j):
-        total = p2f[w, :, pl.ds(j * hw, hw)]
+        total = p2o[w, j]
         arrive(f"t{w}{j}", p2_r.at[w, j])
         for n in range(3):
             total = total + p2_r[w, j, n].astype(F32)
@@ -299,17 +293,17 @@
         if w == 1:
             b_v[where[j]] = value
             for to in same_team:
-                send(b_v.at[where[j]], b_v.at[where[j]], to, "n", keep=False)
+                send(b_v.at[where[j]], b_v.at[where[j]], to, f"n{j}", keep=False)
         else:
             a2_s[j] = value
             for to in even_team:
-                send(a2_s.at[j], b_v.at[where[j]], to, "n", keep=False)
+                send(a2_s.at[j], b_v.at[where[j]], to, f"n{j}", keep=False)
 
     def relay_piece(k):
         a_across[k].wait_recv()
-        relay[k] = share(a_v.at[span(over, blk), pl.ds(k * piece, piece)], mate, "r3" if k == PIECES - 1 else "r")
-
-    early = depth - piece
+        relay[k] = share(a_v.at[span(over, blk), pieces[k]], mate, "rf" if k == final else "r")
+
+    early = SPLIT[final][0] * unit
 
     def add_pieces():
         for c in range(CHUNKS):
@@ -317,7 +311,7 @@
             acc[other_rows, own] = mm(a_v[other_rows, pl.ds(0, early)], b_v[pl.ds(0, early), own])
 
     def add_last():
-        deep = pl.ds(early, piece)
+        deep = pieces[final]
         for c in range(CHUNKS):
             own = pl.ds(c * cw, cw)
             acc[other_rows, own] = acc[other_rows, own] + mm(a_v[other_rows, deep], b_v[deep, own])
@@ -332,6 +326,7 @@
     second_part(0)
     second_part(1)
     relay_piece(0)
+    relay_piece(1)
 
     @pl.when(inner == 1)
     def _():
@@ -339,16 +334,16 @@
 
     @pl.when(core == 1)
     def _():
-        arrive("tf", p2f.at[0])
+        arrive("tf", p2o.at[0])
         for j in range(2):
             third_far(1, j)
             third_far(0, j)
 
-    relay_piece(1)
+    relay_piece(2)
     first((2, 3))
     second_sum(3)
     second_part(2)
-    relay_piece(2)
+    relay_piece(3)
 
     @pl.when(core == 1)
     def _():
@@ -358,25 +353,27 @@
 
     second_join(0)
     second_join(1)
-    relay_piece(3)
+    relay_piece(final)
     arrive("r", a_v.at[block, pl.ds(0, early)])
     add_pieces()
     second(3)
     second_join(2)
-    relay[3].wait_recv()
+    relay[final].wait_recv()
     add_last()
     answers = pl.ds(depth + 2 * rank, rank)
 
-    @pl.when(core == 1)
-    def _():
-        arrive("n", b_v.at[answers, pl.ds(0, (CHUNKS - 1) * cw)])
-
-    @pl.when(core == 0)
-    def _():
-        arrive("n", b_v.at[answers, pl.ds(0, CHUNKS * cw)])
-
-    for c in range(CHUNKS):
-        finish(c)
+    for j in range(2):
+
+        @pl.when(core == 1)
+        def _():
+            arrive(f"n{j}", b_v.at[answers, pl.ds(0, 3 * hw)])
+
+        @pl.when(core == 0)
+        def _():
+            arrive(f"n{j}", b_v.at[answers, pl.ds(0, 4 * hw)])
+
+        finish(2 * j)
+        finish(2 * j + 1)
     assert len(slots) == RECVS and len(places) == FETCHES, (len(slots), len(places))
     for copy in copies:
         copy.wait_send()
@@ -392,7 +389,7 @@
 
     @pl.when(core == 0)
     def _():
-        sent(p2f.at[0])
+        sent(p2o.at[0])
 
 
 def local(right_sides, leaf_inverse, project_factors, correct_factors, *couplings):
@@ -424,7 +421,7 @@
             whole(F32),
             pltpu.VMEM((CHUNKS, 2 * rank, cw), BF),
             whole(F32), whole(BF), whole(BF),
-            pltpu.VMEM((2, rank, cw), F32), pltpu.VMEM((2, 3, rank, cw // 2), BF),
+            whole(F32), whole(BF), pltpu.VMEM((2, 2, rank, cw // 2), F32),
             pltpu.VMEM((2, 2, 3, rank, cw // 2), BF),
             pltpu.VMEM((CHUNKS, 2 * rank, cw), BF),
             pltpu.VMEM((2, 2, 2 * rank, cw // 2), BF),

time: 34.8 us -> 34.2 us (0.983)
  Pallas kernels: 33.3 us -> 32.8 us
    pallas_call x1, Pallas kernels: 33.3 us -> 32.8 us  [local(): pl.pallas_call(kernel, out_shape=jax.ShapeDtypeStruct((rows, cols), BF),...]
where the time goes in v9:
time: 34.2 us; the launch traced here: 34.1 us
  Pallas kernels  32.8 us (96%)
  local copies, waits for them, and re-layouts  1.32 us (4%)
    pallas_call x1, Pallas kernels, local(): pl.pallas_call(kernel, out_shape=jax.ShapeDtypeStruct((rows, cols), BF),...  32.8 us
    unnamed x1, local copies, waits for them, and re-layouts  1.32 us

profile of v9, /device:TPU:0, one launch (start us, length us, event | category | flops | bytes accessed | tf_op | source)
XLA Modules:
  0.0 34.1 jit_solution(362321010191035976)
XLA Ops:
  0.0 32.8 %shard_map.73 = bf16[1024,1024]{1,0:T(8,128)(2,1)S(1)} custom-call(bf16[1024,1024]{1,0:T(8,128)(2,1)} %b_hbm.1, bf16[256,1024]{1,0:T(8,128)(2,1)} %a_hbm.1, bf16[3,1024,128]{2,1,0:T(8,128)(2,1)} %p_hbm.1, bf16[3,1024,128]{2,1,0:T(8,128)(2,1)} %c_hbm.1, bf16[4,64,256]{2,1,0:T(8,128)(2,1)} %w0_hbm.1, bf16[2,64,256]{2,1,0:T(8,128)(2,1)} %w1_hbm.1, ...), custom_call_target="tpu_custom_call" | custom-call | tf_op jit(solution)/shard_map/pallas_call | solution.py:403
  32.8 1.3 %copy.9 = bf16[1024,1024]{1,0:T(8,128)(2,1)} copy(bf16[1024,1024]{1,0:T(8,128)(2,1)S(1)} %shard_map.73) | data formatting | bytes 4194304

commit v10 on v9

--- a/solution.py
+++ b/solution.py
@@ -348,8 +348,8 @@
     @pl.when(core == 1)
     def _():
         for j in range(2):
+            third(0, j)
             third(1, j)
-            third(0, j)
 
     second_join(0)
     second_join(1)

time: 34.2 us -> 33.5 us (0.980)
  Pallas kernels: 32.8 us -> 32.1 us
    pallas_call x1, Pallas kernels: 32.8 us -> 32.1 us  [local(): pl.pallas_call(kernel, out_shape=jax.ShapeDtypeStruct((rows, cols), BF),...]
where the time goes in v10:
time: 33.5 us; the launch traced here: 33.4 us
  Pallas kernels  32.1 us (96%)
  local copies, waits for them, and re-layouts  1.32 us (4%)
    pallas_call x1, Pallas kernels, local(): pl.pallas_call(kernel, out_shape=jax.ShapeDtypeStruct((rows, cols), BF),...  32.1 us
    unnamed x1, local copies, waits for them, and re-layouts  1.32 us

profile of v10, /device:TPU:0, one launch (start us, length us, event | category | flops | bytes accessed | tf_op | source)
XLA Modules:
  0.0 33.4 jit_solution(18163439532545803048)
XLA Ops:
  0.0 32.1 %shard_map.73 = bf16[1024,1024]{1,0:T(8,128)(2,1)S(1)} custom-call(bf16[1024,1024]{1,0:T(8,128)(2,1)} %b_hbm.1, bf16[256,1024]{1,0:T(8,128)(2,1)} %a_hbm.1, bf16[3,1024,128]{2,1,0:T(8,128)(2,1)} %p_hbm.1, bf16[3,1024,128]{2,1,0:T(8,128)(2,1)} %c_hbm.1, bf16[4,64,256]{2,1,0:T(8,128)(2,1)} %w0_hbm.1, bf16[2,64,256]{2,1,0:T(8,128)(2,1)} %w1_hbm.1, ...), custom_call_target="tpu_custom_call" | custom-call | tf_op jit(solution)/shard_map/pallas_call | solution.py:403
  32.1 1.3 %copy.9 = bf16[1024,1024]{1,0:T(8,128)(2,1)} copy(bf16[1024,1024]{1,0:T(8,128)(2,1)S(1)} %shard_map.73) | data formatting | bytes 4194304

commit v11 on v10

--- a/solution.py
+++ b/solution.py
@@ -10,8 +10,8 @@
 SPLIT = ((0, 1), (1, 2), (3, 2), (5, 2), (7, 1))
 UNITS = 8
 ZFIRST = 3
-RECVS = 43
-FETCHES = 7
+RECVS = 37
+FETCHES = 8
 BF = jnp.bfloat16
 F32 = jnp.float32
 
@@ -100,7 +100,8 @@
     half_cols = span(core, half)
     rest_cols = span(1 - core, half)
 
-    la = fetch(a_hbm, a_v.at[block, pl.ds(0, depth)], "a")
+    la = fetch(a_hbm.at[:, rest_cols], a_v.at[block, rest_cols], "a")
+    lo = fetch(a_hbm.at[:, half_cols], a_v.at[block, half_cols], "o")
     lp = [fetch(p_hbm.at[0], p_v.at[:, pl.ds(0, rank)], "p0")]
     [
         fetch(w_hbm.at[lax.div(i, 2 << level)], w_v.at[level, r], "w")
@@ -128,7 +129,8 @@
 
 
     a_mate = share(a_v.at[block, rest_cols], mate, "am")
-    a_across = [share(a_v.at[block, pieces[0]], across, "a0")]
+    lo.wait()
+    a_across = [share(a_v.at[block, pieces[0]], across, "a1")]
     fetched("w", w_v.at[:, r])
     [share(w_v.at[l, r, :, mine[l]], across, "we") for l in range(2)]
     lp[0].wait()
@@ -144,7 +146,7 @@
         q_s[l] = part.astype(BF)
         q_across.append(send(q_s.at[l], q_r.at[l], across, f"q{l}"))
     a_mate2 = share(a_v.at[block, half_cols], mate, "an")
-    w_mate = share(w_v.at[:, r], mate, "wm")
+    w_mate = share(w_v.at[:, r], mate, "wg")
     [share(w_v.at[l, r, :, span(1 - sides[l], rank)], across, "wl") for l in range(2)]
     share(w_v.at[2, r], across, "wl")
     for k in range(1, len(SPLIT)):
@@ -153,7 +155,7 @@
     fetched("c", a_v.at[:, pl.ds(depth, LEVELS * rank)])
     for n, (l, k) in enumerate(((1, 0), (2, 0), (2, 1))):
         g_v[n, :, mine[0]] = mm(pt_v[l], a_v[:, pl.ds(depth + k * rank, rank)]).astype(BF)
-    g_send = share(g_v.at[:, :, mine[0]], sib, "g")
+    g_send = share(g_v.at[:, :, mine[0]], sib, "wg")
 
     over = flip(r, 2)
     arrive("we", w_v.at[0, r])
@@ -189,8 +191,8 @@
         st0[c, mine[0], :] = project(0, c).astype(BF)
         send0(c)
 
-    w_mate.wait_recv()
-    g_send.wait_recv()
+    both = (LEVELS * w0_hbm.shape[1] * w0_hbm.shape[2] + 3 * rank * rank) // cols
+    arrive("wg", b_v.at[pl.ds(0, both)])
     arrive("re", w_v.at[0, r])
     w_cols = w_v[0, :, :, mine[0]].reshape(2 * rank, rank)
     for n in range(2):
@@ -200,7 +202,7 @@
     gs_send = share(gs_v.at[:, mine[1]], near, "gs")
 
     def cross(c):
-        z1[c] = send(p1_s.at[c], st1.at[c, mine[1], :], near, f"z{c}")
+        z1[c] = send(p1_s.at[c], st1.at[c, mine[1], :], near, f"z{max(c, 1)}")
 
     gather_q(1)
     for c in range(CHUNKS):
@@ -264,14 +266,20 @@
         b_v[pl.ds(depth + rank, rank), pl.ds(c * cw, cw)] = (-mm(answer_rows(1), st1[c])).astype(BF)
 
     def second_part(c):
-        z1[c].wait_recv()
+        if c == 0:
+            arrive("z1", st1.at[pl.ds(0, 2), mine[1], :])
+        elif c > 1:
+            z1[c].wait_recv()
         part = mm(answer_rows(1), st1[c])
         uf[c] = part
         u_s[c] = part.astype(BF)
-        u1[c] = send(u_s.at[c], u_r.at[c], sib, f"u{c}")
+        u1[c] = send(u_s.at[c], u_r.at[c], sib, f"u{max(c, 1)}")
 
     def second_join(c):
-        u1[c].wait_recv()
+        if c == 0:
+            arrive("u1", u_r.at[pl.ds(0, 2)])
+        elif c > 1:
+            u1[c].wait_recv()
         b_v[pl.ds(depth + rank, rank), pl.ds(c * cw, cw)] = (-(uf[c] + u_r[c].astype(F32))).astype(BF)
 
     where = [(pl.ds(depth + 2 * rank, rank), span(4 * j + spot, hw)) for j in range(2)]
@@ -285,10 +293,11 @@
             total = total + p2_r[w, j, n].astype(F32)
         st2[w, j, mine[2], :] = total.astype(BF)
         ours = st2.at[w, j, mine[2], :]
-        send(ours, ours, far, f"f{w}{j}", keep=False)
+        send(ours, ours, far, f"f{j}", keep=False)
 
     def third(w, j):
-        arrive(f"f{w}{j}", st2.at[w, j, mine[2], :])
+        if w == 0:
+            arrive(f"f{j}", st2.at[:, j, mine[2], :])
         value = (-mm(answer_rows(2), st2[w, j])).astype(BF)
         if w == 1:
             b_v[where[j]] = value
@@ -300,7 +309,10 @@
                 send(a2_s.at[j], b_v.at[where[j]], to, f"n{j}", keep=False)
 
     def relay_piece(k):
-        a_across[k].wait_recv()
+        if k == 1:
+            arrive("a1", a_v.at[block, pl.ds(0, SPLIT[2][0] * unit)])
+        elif k > 1:
+            a_across[k].wait_recv()
         relay[k] = share(a_v.at[span(over, blk), pieces[k]], mate, "rf" if k == final else "r")
 
     early = SPLIT[final][0] * unit
@@ -325,8 +337,8 @@
     first((0, 1))
     second_part(0)
     second_part(1)
+    relay_piece(1)
     relay_piece(0)
-    relay_piece(1)
 
     @pl.when(inner == 1)
     def _():

time: 33.5 us -> 33.5 us (level)
  no operation moved by 1% of the time
where the time goes in v11:
time: 33.5 us; the launch traced here: 33.3 us
  Pallas kernels  32 us (96%)
  local copies, waits for them, and re-layouts  1.32 us (4%)
    pallas_call x1, Pallas kernels, local(): pl.pallas_call(kernel, out_shape=jax.ShapeDtypeStruct((rows, cols), BF),...  32 us
    unnamed x1, local copies, waits for them, and re-layouts  1.32 us

profile of v11, /device:TPU:0, one launch (start us, length us, event | category | flops | bytes accessed | tf_op | source)
XLA Modules:
  0.0 33.3 jit_solution(17981511998086391633)
XLA Ops:
  0.0 32.0 %shard_map.73 = bf16[1024,1024]{1,0:T(8,128)(2,1)S(1)} custom-call(bf16[1024,1024]{1,0:T(8,128)(2,1)} %b_hbm.1, bf16[256,1024]{1,0:T(8,128)(2,1)} %a_hbm.1, bf16[3,1024,128]{2,1,0:T(8,128)(2,1)} %p_hbm.1, bf16[3,1024,128]{2,1,0:T(8,128)(2,1)} %c_hbm.1, bf16[4,64,256]{2,1,0:T(8,128)(2,1)} %w0_hbm.1, bf16[2,64,256]{2,1,0:T(8,128)(2,1)} %w1_hbm.1, ...), custom_call_target="tpu_custom_call" | custom-call | tf_op jit(solution)/shard_map/pallas_call | solution.py:415
  32.0 1.3 %copy.9 = bf16[1024,1024]{1,0:T(8,128)(2,1)} copy(bf16[1024,1024]{1,0:T(8,128)(2,1)S(1)} %shard_map.73) | data formatting | bytes 4194304

commit v12 on v11

--- a/solution.py
+++ b/solution.py
@@ -348,8 +348,8 @@
     def _():
         arrive("tf", p2o.at[0])
         for j in range(2):
-            third_far(1, j)
-            third_far(0, j)
+            for w in ((1, 0) if j == 0 else (0, 1)):
+                third_far(w, j)
 
     relay_piece(2)
     first((2, 3))

time: 33.5 us -> 33.5 us (level)
  no operation moved by 1% of the time
where the time goes in v12:
time: 33.5 us; the launch traced here: 33.3 us
  Pallas kernels  32 us (96%)
  local copies, waits for them, and re-layouts  1.32 us (4%)
    pallas_call x1, Pallas kernels, local(): pl.pallas_call(kernel, out_shape=jax.ShapeDtypeStruct((rows, cols), BF),...  32 us
    unnamed x1, local copies, waits for them, and re-layouts  1.32 us

profile of v12, /device:TPU:0, one launch (start us, length us, event | category | flops | bytes accessed | tf_op | source)
XLA Modules:
  0.0 33.3 jit_solution(16323232493738571843)
XLA Ops:
  0.0 32.0 %shard_map.73 = bf16[1024,1024]{1,0:T(8,128)(2,1)S(1)} custom-call(bf16[1024,1024]{1,0:T(8,128)(2,1)} %b_hbm.1, bf16[256,1024]{1,0:T(8,128)(2,1)} %a_hbm.1, bf16[3,1024,128]{2,1,0:T(8,128)(2,1)} %p_hbm.1, bf16[3,1024,128]{2,1,0:T(8,128)(2,1)} %c_hbm.1, bf16[4,64,256]{2,1,0:T(8,128)(2,1)} %w0_hbm.1, bf16[2,64,256]{2,1,0:T(8,128)(2,1)} %w1_hbm.1, ...), custom_call_target="tpu_custom_call" | custom-call | tf_op jit(solution)/shard_map/pallas_call | solution.py:415
  32.0 1.3 %copy.9 = bf16[1024,1024]{1,0:T(8,128)(2,1)} copy(bf16[1024,1024]{1,0:T(8,128)(2,1)S(1)} %shard_map.73) | data formatting | bytes 4194304
